TPU v7x, 16 devices: a whole 2x2x2 slice. The times are simulated.
16 devices in a mesh: w: 2 (over z), h: 8 (over y, x, core).
Axes of the slice: x: 2, y: 2, z: 2, core: 2. Of those that a mesh axis runs over, the one named last changes fastest.
Arguments:
- x: bfloat16 [1, 64, 512, 640], P(None, 'h', 'w')
- w1: bfloat16 [3, 3, 640, 640], replicated
- gamma: float32 [640], replicated
- beta: float32 [640], replicated
- w2: bfloat16 [3, 3, 640, 640], replicated
- g: bfloat16 [1, 64, 512, 640], P(None, 'h', 'w')
Outputs:
- output 1: bfloat16 [1, 64, 512, 640], P(None, 'h', 'w')
- output 2: bfloat16 [1, 64, 512, 640], P(None, 'h', 'w')
- output 3: float32 [3, 3, 640, 640], replicated
- output 4: float32 [3, 3, 640, 640], replicated
- output 5: float32 [640], replicated
- output 6: float32 [640], replicated
All inputs are finite; a program needn't handle non-finite values.
Results may differ from a plain program's by a relative error of at most 0.00136563.
Values are sent between devices in bfloat16 or wider.
A program may use at most 1 GiB of HBM per device.

v0:
```python
import jax
import jax.numpy as jnp
from jax import lax
from jax.sharding import PartitionSpec as P

GROUPS = 32
EPS = 1e-5
DN = ('NHWC', 'HWIO', 'NHWC')


def _conv(up, w):
    return lax.conv_general_dilated(up, w, (1, 1), 'VALID', dimension_numbers=DN, preferred_element_type=jnp.float32)


def _flip_t(w):
    return jnp.flip(w, (0, 1)).transpose(0, 1, 3, 2)


def _wgrad(up, v):
    th, tw = v.shape[1], v.shape[2]
    return jnp.stack([jnp.stack([jnp.einsum('bhwc,bhwo->co', up[:, a:a + th, b:b + tw], v, preferred_element_type=jnp.float32) for b in range(3)]) for a in range(3)])


def _edge(u, axis, name, n):
    lo = lax.slice_in_dim(u, 0, 1, axis=axis)
    hi = lax.slice_in_dim(u, u.shape[axis] - 1, u.shape[axis], axis=axis)
    if n == 1:
        prev = jnp.zeros_like(lo)
        nxt = jnp.zeros_like(lo)
    else:
        prev = lax.ppermute(hi, name, [(i, i + 1) for i in range(n - 1)])
        nxt = lax.ppermute(lo, name, [(i + 1, i) for i in range(n - 1)])
    return jnp.concatenate([prev, u, nxt], axis=axis)


def solution(mesh):
    nh, nw = mesh.shape['h'], mesh.shape['w']
    tile = P(None, 'h', 'w', None)

    def halo(u):
        return _edge(_edge(u, 1, 'h', nh), 2, 'w', nw)

    def body(x, w1, gamma, beta, w2, g):
        nb, th, tw, c = x.shape
        cg = c // GROUPS
        cnt = th * nh * tw * nw * cg
        xp = halo(x)
        a = _conv(xp, w1).astype(jnp.bfloat16).astype(jnp.float32)
        s = jnp.stack([a.sum((1, 2)), (a * a).sum((1, 2))])
        s = lax.psum(s.reshape(2, nb, GROUPS, cg).sum(-1), ('h', 'w')) / cnt
        rstd_g = lax.rsqrt(s[1] - s[0] * s[0] + EPS)
        mean = jnp.repeat(s[0], cg, axis=-1)[:, None, None, :]
        rstd = jnp.repeat(rstd_g, cg, axis=-1)[:, None, None, :]
        xhatv = (a - mean) * rstd
        zf, gelu_vjp = jax.vjp(lambda n: jax.nn.gelu(n, approximate=True), xhatv * gamma + beta)
        z = zf.astype(jnp.bfloat16)
        zp = halo(z)
        y = (_conv(zp, w2) + x.astype(jnp.float32)).astype(jnp.bfloat16)
        gp = halo(g)
        dz = _conv(gp, _flip_t(w2))
        dw2 = lax.psum(_wgrad(zp, g), ('h', 'w'))
        (dn,) = gelu_vjp(dz)
        t = lax.psum(jnp.stack([(dn * xhatv).sum((1, 2)), dn.sum((1, 2))]), ('h', 'w'))
        dgamma = t[0].sum(0)
        dbeta = t[1].sum(0)
        u = jnp.repeat((t * gamma).reshape(2, nb, GROUPS, cg).sum(-1) / cnt, cg, axis=-1)[:, :, None, None, :]
        da = (rstd * (dn * gamma - u[1] - xhatv * u[0])).astype(jnp.bfloat16)
        dap = halo(da)
        dx = (_conv(dap, _flip_t(w1)) + g.astype(jnp.float32)).astype(jnp.bfloat16)
        dw1 = lax.psum(_wgrad(xp, da), ('h', 'w'))
        return y, dx, dw1, dw2, dgamma, dbeta

    return jax.shard_map(body, mesh=mesh, in_specs=(tile, P(), P(), P(), P(), tile), out_specs=(tile, tile, P(), P(), P(), P()), check_vma=False)
```

profile of v0, /device:TPU:0, one launch (start us, length us, event | category | flops | bytes accessed | tf_op | source)
XLA Modules:
  0.0 699.7 jit_solution(11487217228432351941)
XLA Ops:
  7.2 3.0 copy.52
  11.5 3.3 collective-permute-start
  16.8 5.2 collective-permute-start.8
  32.1 4.5 collective-permute-start.2
  44.0 4.5 collective-permute-start.10
  52.0 7.1 %maximum_bitcast_fusion = bf16[10,1,258,640]{2,3,0,1:T(8,128)(2,1)} fusion(bf16[1,10,1,640]{2,3,1,0:T(8,128)(2,1)} %copy.58, bf16[1,1,256,640]{2,3,1,0:T(8,128)(2,1)S(1)} %collective-permute-done.1, bf16[1,8,256,640]{2,3,1,0:T(8,128)(2,1)S(1)} %copy.52, bf16[1,1,256,640]{2,3,1,0:T(8,128)(2,1)S(1)} %collective-permute-done, bf16[1,10,1,640]{2,3,1,0:T(8,128)(2,1)} %copy.57), kind=kLoop, calls=%fused_computation.44 | loop fusion | flops 16512000 | bytes 6604800 | tf_op jit(solution)/shard_map/concatenate | solution.py:33
  59.1 7.8 %copy.104 = bf16[10,1,258,640]{3,2,0,1:T(8,128)(2,1)} copy(bf16[10,1,258,640]{2,3,0,1:T(8,128)(2,1)} %maximum_bitcast_fusion) | data formatting | bytes 6604800
  66.9 4.0 pad.clone
  70.9 5.7 reshape.184
  79.3 24.1 %fusion.10 = (f32[640]{0:T(1024)S(1)}, f32[640]{0:T(1024)S(1)}, bf16[8,8,33,640]{3,1,2,0:T(8,128)(2,1)}) fusion(pred[8,33]{0,1:T(8,128)(4,1)S(1)} %copy-done.29, bf16[3,3,640,640]{3,2,1,0:T(8,128)(2,1)} %param.7, bf16[10,1,7,2,640]{4,2,3,0,1:T(8,128)(2,1)S(1)} %slice.200, bf16[10,1,8,33,640]{4,2,3,0,1:T(8,128)(2,1)S(1)} %copy.61), kind=kOutput, calls=%fused_computation.18 | convolution fusion | flops 15592916992 | bytes 13639944 | tf_op jit(solution)/shard_map/conv_general_dilated | solution.py:12
  103.8 33.6 %psum.28 = f32[2,1,32]{2,0,1:T(2,128)S(1)} all-reduce(f32[2,1,32]{2,0,1:T(2,128)S(1)} %bitcast.333), channel_id=1, replica_groups=mesh['w'=2,'h'=8] {'h','w'}, use_global_device_ids=true, to_apply=%region_3.0 | all-reduce | flops 64 | bytes 512 | tf_op jit(solution)/shard_map/psum | solution.py:50
  142.7 5.7 reshape.202
  151.4 30.4 %fusion.27 = (f32[640]{0:T(1024)S(1)}, f32[640]{0:T(1024)S(1)}, f32[8,8,33,640]{3,1,2,0:T(8,128)}) fusion(bf16[8,8,33,640]{3,1,2,0:T(8,128)(2,1)S(1)} %copy-done.15, f32[640]{0:T(1024)S(1)} %broadcast_in_dim.26, f32[640]{0:T(1024)S(1)} %broadcast_in_dim.24, pred[8,33]{0,1:T(8,128)(4,1)S(1)} %copy-done.29, f32[640]{0:T(1024)S(1)} %copy-done.28, ...), kind=kOutput, calls=%fused_computation.35 | convolution fusion | flops 15622653952 | bytes 19056904 | tf_op jit(solution)/shard_map/conv_general_dilated | solution.py:12
  181.8 33.0 %psum.29 = f32[2,1,640]{2,0,1:T(2,128)S(1)} all-reduce(f32[2,1,640]{2,0,1:T(2,128)S(1)} %pad_maximum_fusion.13), channel_id=1, replica_groups=mesh['w'=2,'h'=8] {'h','w'}, use_global_device_ids=true, to_apply=%region_6.7 | all-reduce | flops 1280 | bytes 10240 | tf_op jit(solution)/shard_map/psum | solution.py:63
  215.4 5.9 fusion.25
  226.4 3.7 maximum_maximum_fusion
  230.2 3.6 fusion.157
  233.7 3.6 fusion.140
  237.4 3.4 fusion.149
  240.8 3.4 fusion.132
  244.2 3.6 fusion.146
  247.8 3.6 fusion.122
  251.4 3.9 fusion.143
  262.7 3.5 slice.203
  266.2 4.7 copy.101
  278.1 4.0 collective-permute-start.4
  282.1 3.9 fusion.152
  292.3 4.1 maximum_bitcast_fusion.2
  296.4 11.9 %pad_maximum_fusion = f32[3,3,640,640]{3,2,1,0:T(8,128)} fusion(f32[1,3,640,640]{3,2,1,0:T(8,128)} %maximum_bitcast_fusion.4, f32[1,3,640,640]{3,2,1,0:T(8,128)} %get-tuple-element.55, f32[1,3,640,640]{3,2,1,0:T(8,128)} %get-tuple-element.54), kind=kLoop, calls=%fused_computation | loop fusion | flops 7372800 | bytes 29491200 | tf_op jit(solution)/shard_map/stack | solution.py:21
  308.2 5.1 fusion.127
  323.2 4.8 collective-permute-start.6
  328.0 5.2 fusion.180
  333.3 4.3 fusion.163
  341.0 5.9 maximum_maximum_fusion.1
  368.4 12.1 %pad_maximum_fusion.1 = f32[3,3,640,640]{3,2,1,0:T(8,128)} fusion(f32[1,3,640,640]{3,2,1,0:T(8,128)} %maximum_bitcast_fusion.7, f32[1,3,640,640]{3,2,1,0:T(8,128)} %maximum_bitcast_fusion.6, f32[1,3,640,640]{3,2,1,0:T(8,128)} %maximum_bitcast_fusion.5), kind=kLoop, calls=%fused_computation.1 | loop fusion | flops 7372800 | bytes 29491200 | tf_op jit(solution)/shard_map/stack | solution.py:21
  385.8 3.4 collective-permute-start.12
  394.9 4.5 collective-permute-start.14
  399.4 6.6 maximum_bitcast_fusion.1
  406.1 7.9 %copy.105 = bf16[10,1,258,640]{3,2,0,1:T(8,128)(2,1)} copy(bf16[10,1,258,640]{2,3,0,1:T(8,128)(2,1)} %maximum_bitcast_fusion.1) | data formatting | bytes 6604800
  413.9 3.9 pad.2.clone
  417.9 5.8 reshape.197
  426.3 25.1 %broadcast_select_fusion.1 = f32[8,8,33,640]{3,1,2,0:T(8,128)S(1)} fusion(pred[8,33]{0,1:T(8,128)(4,1)S(1)} %copy-done.30, bf16[3,3,640,640]{3,2,1,0:T(8,128)(2,1)} %param.10, bf16[10,1,7,2,640]{4,2,3,0,1:T(8,128)(2,1)S(1)} %slice.208, bf16[10,1,8,33,640]{4,2,3,0,1:T(8,128)(2,1)S(1)} %copy.74), kind=kOutput, calls=%fused_computation.85 | convolution fusion | flops 15583457280 | bytes 16338184 | tf_op jit(solution)/shard_map/conv_general_dilated | solution.py:12
  457.9 5.0 maximum_bitcast_fusion.9
  464.9 5.8 reshape.215
  473.3 33.3 %broadcast_select_fusion = f32[8,8,33,640]{3,1,2,0:T(8,128)S(1)} fusion(pred[8,33]{0,1:T(8,128)(4,1)S(1)} %copy-done.30, bf16[3,3,640,640]{3,2,1,0:T(8,128)(2,1)} %param.7, bf16[10,1,7,2,640]{4,2,3,0,1:T(8,128)(2,1)S(1)} %slice.218, bf16[10,1,8,33,640]{4,2,3,0,1:T(8,128)(2,1)S(1)} %copy.84), kind=kOutput, calls=%fused_computation.84 | convolution fusion | flops 15583457280 | bytes 16338184 | tf_op jit(solution)/shard_map/conv_general_dilated | solution.py:12
  512.2 156.9 %all-reduce.3.cloned.1.call-done = (f32[3,3,640,640]{3,2,1,0:T(8,128)}, f32[3,3,640,640]{3,2,1,0:T(8,128)}) async-done(((f32[3,3,640,640]{3,2,1,0:T(8,128)}, f32[3,3,640,640]{3,2,1,0:T(8,128)}), (f32[3,3,640,640]{3,2,1,0:T(8,128)}, f32[3,3,640,640]{3,2,1,0:T(8,128)})) %all-reduce.3.cloned.1.call-update) | async-done | bytes 29491216 | tf_op jit(solution)/shard_map/psum | solution.py:70
  669.1 11.6 %copy.150 = f32[3,3,640,640]{3,2,1,0:T(8,128)} copy(f32[3,3,640,640]{3,2,1,0:T(8,128)} %get-tuple-element.58) | data formatting | bytes 29491200
  680.8 11.6 %copy.151 = f32[3,3,640,640]{3,2,1,0:T(8,128)} copy(f32[3,3,640,640]{3,2,1,0:T(8,128)} %get-tuple-element.59) | data formatting | bytes 29491200
  (177 shorter events, 126.6 us)
Async XLA Ops:
  7.2 662.0 %all-reduce.3.cloned.1.call-start = ((), (), s32[]{:S(2)}) async-start(), calls=%async_computation | async-start | bytes 58982400 | tf_op jit(solution)/shard_map/psum | solution.py:70
  10.2 13.1 %collective-permute-start.1 = (bf16[1,1,256,640]{2,3,1,0:T(8,128)(2,1)S(1)}, bf16[1,1,256,640]{2,3,1,0:T(8,128)(2,1)S(1)}, u32[]{:S(2)}, u32[]{:S(2)}) collective-permute-start(bf16[1,1,256,640]{2,3,1,0:T(8,128)(2,1)S(1)} %get-tuple-element.47), channel_id=1, source_target_pairs={{1,0},{2,1},{3,2},{4,3},{5,4},{6,5},{7,6},{9,8},{10,9},{11,10},{12... | collective-permute-start | bytes 983048 | tf_op jit(solution)/shard_map/ppermute | solution.py:32
  11.5 11.8 %collective-permute-start = (bf16[1,1,256,640]{2,3,1,0:T(8,128)(2,1)S(1)}, bf16[1,1,256,640]{2,3,1,0:T(8,128)(2,1)S(1)}, u32[]{:S(2)}, u32[]{:S(2)}) collective-permute-start(bf16[1,1,256,640]{2,3,1,0:T(8,128)(2,1)S(1)} %get-tuple-element.46), channel_id=1, source_target_pairs={{0,1},{1,2},{2,3},{3,4},{4,5},{5,6},{6,7},{8,9},{9,10},{10,11},{11... | collective-permute-start | bytes 983048 | tf_op jit(solution)/shard_map/ppermute | solution.py:31
  16.8 19.9 %collective-permute-start.8 = (bf16[1,1,256,640]{3,2,1,0:T(8,128)(2,1)}, bf16[1,1,256,640]{3,2,1,0:T(8,128)(2,1)}, u32[]{:S(2)}, u32[]{:S(2)}) collective-permute-start(bf16[1,1,256,640]{3,2,1,0:T(8,128)(2,1)} %get-tuple-element.45), channel_id=1, source_target_pairs={{0,1},{1,2},{2,3},{3,4},{4,5},{5,6},{6,7},{8,9},{9,10},{10,11},{11... | collective-permute-start | bytes 983048 | tf_op jit(solution)/shard_map/ppermute | solution.py:31
  22.0 17.9 %collective-permute-start.9 = (bf16[1,1,256,640]{3,2,1,0:T(8,128)(2,1)}, bf16[1,1,256,640]{3,2,1,0:T(8,128)(2,1)}, u32[]{:S(2)}, u32[]{:S(2)}) collective-permute-start(bf16[1,1,256,640]{3,2,1,0:T(8,128)(2,1)} %get-tuple-element.44), channel_id=1, source_target_pairs={{1,0},{2,1},{3,2},{4,3},{5,4},{6,5},{7,6},{9,8},{10,9},{11,10},{12... | collective-permute-start | bytes 983048 | tf_op jit(solution)/shard_map/ppermute | solution.py:32
  28.5 20.1 %collective-permute-start.3 = (bf16[1,10,1,640]{3,1,2,0:T(8,128)(2,1)S(1)}, bf16[1,10,1,640]{3,1,2,0:T(8,128)(2,1)S(1)}, u32[]{:S(2)}, u32[]{:S(2)}) collective-permute-start(bf16[1,10,1,640]{3,1,2,0:T(8,128)(2,1)S(1)} %copy.56), channel_id=1, source_target_pairs={{8,0},{9,1},{10,2},{11,3},{12,4},{13,5},{14,6},{15,7}} | collective-permute-start | bytes 38408 | tf_op jit(solution)/shard_map/ppermute | solution.py:32
  32.1 18.2 %collective-permute-start.2 = (bf16[1,10,1,640]{3,1,2,0:T(8,128)(2,1)S(1)}, bf16[1,10,1,640]{3,1,2,0:T(8,128)(2,1)S(1)}, u32[]{:S(2)}, u32[]{:S(2)}) collective-permute-start(bf16[1,10,1,640]{3,1,2,0:T(8,128)(2,1)S(1)} %copy.55), channel_id=1, source_target_pairs={{0,8},{1,9},{2,10},{3,11},{4,12},{5,13},{6,14},{7,15}} | collective-permute-start | bytes 38408 | tf_op jit(solution)/shard_map/ppermute | solution.py:31
  41.0 1.7 copy-start.14
  42.7 95.1 %collective-permute-start.11 = (bf16[1,10,1,640]{3,2,1,0:T(2,128)(2,1)S(1)}, bf16[1,10,1,640]{3,2,1,0:T(2,128)(2,1)S(1)}, u32[]{:S(2)}, u32[]{:S(2)}) collective-permute-start(bf16[1,10,1,640]{3,2,1,0:T(2,128)(2,1)S(1)} %get-tuple-element.33), channel_id=1, source_target_pairs={{8,0},{9,1},{10,2},{11,3},{12,4},{13,5},{14,6},{15,7}} | collective-permute-start | bytes 38408 | tf_op jit(solution)/shard_map/ppermute | solution.py:32
  44.0 93.8 %collective-permute-start.10 = (bf16[1,10,1,640]{3,2,1,0:T(2,128)(2,1)S(1)}, bf16[1,10,1,640]{3,2,1,0:T(2,128)(2,1)S(1)}, u32[]{:S(2)}, u32[]{:S(2)}) collective-permute-start(bf16[1,10,1,640]{3,2,1,0:T(2,128)(2,1)S(1)} %get-tuple-element.32), channel_id=1, source_target_pairs={{0,8},{1,9},{2,10},{3,11},{4,12},{5,13},{6,14},{7,15}} | collective-permute-start | bytes 38408 | tf_op jit(solution)/shard_map/ppermute | solution.py:31
  76.6 2.7 copy-start.29
  148.4 3.0 copy-start.15
  148.4 3.0 copy-start.27
  148.4 3.0 copy-start.28
  224.5 1.4 copy-start.3
  224.5 1.9 copy-start.4
  226.4 24.9 %copy-start.12 = (bf16[8,1,256,640]{3,0,2,1:T(8,128)(2,1)}, bf16[8,1,256,640]{3,0,2,1:T(8,128)(2,1)S(1)}, u32[]{:S(2)}) copy-start(bf16[8,1,256,640]{3,0,2,1:T(8,128)(2,1)S(1)} %slice.215) | copy-start | bytes 7864324
  244.2 3.6 copy-start.10
  261.4 51.9 %collective-permute-start.5 = (bf16[1,1,256,640]{2,3,1,0:T(8,128)(2,1)}, bf16[1,1,256,640]{2,3,1,0:T(8,128)(2,1)}, u32[]{:S(2)}, u32[]{:S(2)}) collective-permute-start(bf16[1,1,256,640]{2,3,1,0:T(8,128)(2,1)} %copy.102), channel_id=1, source_target_pairs={{1,0},{2,1},{3,2},{4,3},{5,4},{6,5},{7,6},{9,8},{10,9},{11,10},{12... | collective-permute-start | bytes 983048 | tf_op jit(solution)/shard_map/ppermute | solution.py:32
  278.1 8.0 %copy-start.22 = (f32[1,640,640]{2,1,0:T(8,128)S(1)}, f32[1,640,640]{2,1,0:T(8,128)}, u32[]{:S(2)}) copy-start(f32[1,640,640]{2,1,0:T(8,128)} %fusion.157) | copy-start | bytes 4915204
  278.1 8.0 %copy-start.23 = (f32[1,640,640]{2,1,0:T(8,128)S(1)}, f32[1,640,640]{2,1,0:T(8,128)}, u32[]{:S(2)}) copy-start(f32[1,640,640]{2,1,0:T(8,128)} %fusion.149) | copy-start | bytes 4915204
  278.1 35.3 %collective-permute-start.4 = (bf16[1,1,256,640]{2,3,1,0:T(8,128)(2,1)}, bf16[1,1,256,640]{2,3,1,0:T(8,128)(2,1)}, u32[]{:S(2)}, u32[]{:S(2)}) collective-permute-start(bf16[1,1,256,640]{2,3,1,0:T(8,128)(2,1)} %copy.100), channel_id=1, source_target_pairs={{0,1},{1,2},{2,3},{3,4},{4,5},{5,6},{6,7},{8,9},{9,10},{10,11},{11... | collective-permute-start | bytes 983048 | tf_op jit(solution)/shard_map/ppermute | solution.py:31
  286.1 2.9 copy-start.13
  288.9 2.2 copy-start.17
  288.9 2.2 copy-start.18
  288.9 2.4 copy-start.19
  288.9 2.9 copy-start.20
  288.9 3.4 copy-start.21
  296.4 11.9 %copy-start = (bf16[8,1,256,640]{2,3,0,1:T(8,128)(2,1)S(1)}, bf16[8,1,256,640]{2,3,0,1:T(8,128)(2,1)}, u32[]{:S(2)}) copy-start(bf16[8,1,256,640]{2,3,0,1:T(8,128)(2,1)} %copy.101) | copy-start | bytes 7864324
  319.6 18.0 %collective-permute-start.7 = (bf16[1,10,1,640]{3,1,2,0:T(8,128)(2,1)S(1)}, bf16[1,10,1,640]{3,1,2,0:T(8,128)(2,1)S(1)}, u32[]{:S(2)}, u32[]{:S(2)}) collective-permute-start(bf16[1,10,1,640]{3,1,2,0:T(8,128)(2,1)S(1)} %copy.69), channel_id=1, source_target_pairs={{8,0},{9,1},{10,2},{11,3},{12,4},{13,5},{14,6},{15,7}} | collective-permute-start | bytes 38408 | tf_op jit(solution)/shard_map/ppermute | solution.py:32
  323.2 10.0 %copy-start.7 = (bf16[1,8,256,640]{3,2,1,0:T(8,128)(2,1)S(1)}, bf16[1,8,256,640]{3,2,1,0:T(8,128)(2,1)}, u32[]{:S(2)}) copy-start(bf16[1,8,256,640]{3,2,1,0:T(8,128)(2,1)} %param.11) | copy-start | bytes 7864324
  323.2 16.0 %collective-permute-start.6 = (bf16[1,10,1,640]{3,1,2,0:T(8,128)(2,1)S(1)}, bf16[1,10,1,640]{3,1,2,0:T(8,128)(2,1)S(1)}, u32[]{:S(2)}, u32[]{:S(2)}) collective-permute-start(bf16[1,10,1,640]{3,1,2,0:T(8,128)(2,1)S(1)} %copy.68), channel_id=1, source_target_pairs={{0,8},{1,9},{2,10},{3,11},{4,12},{5,13},{6,14},{7,15}} | collective-permute-start | bytes 38408 | tf_op jit(solution)/shard_map/ppermute | solution.py:31
  341.0 6.0 copy-start.8
  358.3 2.2 copy-start.25
  360.5 2.5 copy-start.16
  363.1 2.7 copy-start.24
  380.5 5.0 copy-start.26
  384.2 7.8 %collective-permute-start.13 = (bf16[1,1,256,640]{3,2,1,0:T(8,128)(2,1)}, bf16[1,1,256,640]{3,2,1,0:T(8,128)(2,1)}, u32[]{:S(2)}, u32[]{:S(2)}) collective-permute-start(bf16[1,1,256,640]{3,2,1,0:T(8,128)(2,1)} %slice.217), channel_id=1, source_target_pairs={{1,0},{2,1},{3,2},{4,3},{5,4},{6,5},{7,6},{9,8},{10,9},{11,10},{12... | collective-permute-start | bytes 983048 | tf_op jit(solution)/shard_map/ppermute | solution.py:32
  385.8 13.7 %copy-start.5 = (bf16[1,10,1,640]{2,3,1,0:T(8,128)(2,1)S(1)}, bf16[1,10,1,640]{2,3,1,0:T(8,128)(2,1)}, u32[]{:S(2)}) copy-start(bf16[1,10,1,640]{2,3,1,0:T(8,128)(2,1)} %copy.71) | copy-start | bytes 38404
  385.8 13.7 %copy-start.6 = (bf16[1,10,1,640]{2,3,1,0:T(8,128)(2,1)S(1)}, bf16[1,10,1,640]{2,3,1,0:T(8,128)(2,1)}, u32[]{:S(2)}) copy-start(bf16[1,10,1,640]{2,3,1,0:T(8,128)(2,1)} %copy.70) | copy-start | bytes 38404
  385.8 6.2 collective-permute-start.12
  391.3 1.5 copy-start.1
  393.6 63.5 %collective-permute-start.15 = (bf16[1,10,1,640]{3,2,1,0:T(2,128)(2,1)S(1)}, bf16[1,10,1,640]{3,2,1,0:T(2,128)(2,1)S(1)}, u32[]{:S(2)}, u32[]{:S(2)}) collective-permute-start(bf16[1,10,1,640]{3,2,1,0:T(2,128)(2,1)S(1)} %get-tuple-element.31), channel_id=1, source_target_pairs={{8,0},{9,1},{10,2},{11,3},{12,4},{13,5},{14,6},{15,7}} | collective-permute-start | bytes 38408 | tf_op jit(solution)/shard_map/ppermute | solution.py:32
  394.9 62.2 %collective-permute-start.14 = (bf16[1,10,1,640]{3,2,1,0:T(2,128)(2,1)S(1)}, bf16[1,10,1,640]{3,2,1,0:T(2,128)(2,1)S(1)}, u32[]{:S(2)}, u32[]{:S(2)}) collective-permute-start(bf16[1,10,1,640]{3,2,1,0:T(2,128)(2,1)S(1)} %get-tuple-element.30), channel_id=1, source_target_pairs={{0,8},{1,9},{2,10},{3,11},{4,12},{5,13},{6,14},{7,15}} | collective-permute-start | bytes 38408 | tf_op jit(solution)/shard_map/ppermute | solution.py:31
  423.6 2.7 copy-start.30
  451.5 1.7 copy-start.11
  455.2 2.7 copy-start.2
  506.7 1.7 copy-start.9
Sparse Core Ops, SparseCore 0:
  380.7 288.3 all-reduce.2
where the time goes:
time: 708 us; the launch traced here: 700 us
  matrix products  172 us (24%)
  local copies, waits for them, and re-layouts  161 us (23%)
  waiting for transfers between devices  157 us (22%)
  other arithmetic  82.4 us (12%)
  blocking collectives  66.6 us (9%)
  starting transfers between devices  44.7 us (6%)
  between operations  15.2 us (2%)
    psum x1, waiting for transfers between devices, body(): dw1 = lax.psum(_wgrad(xp, da), ('h', 'w'))  157 us
    conv_general_dilated x4, matrix products, _conv(): lax.conv_general_dilated(up, w, (1, 1), 'VALID', dimension_numbers=DN, pr...  113 us
    unnamed x75, local copies, waits for them, and re-layouts  67.4 us
    dot_general x18, matrix products, _wgrad(): jnp.einsum('bhwc,bhwo->co', up[:, a:a + th, b:b + tw], v, preferred_eleme...  59.3 us
    another operation x7, other arithmetic, _wgrad(): jnp.stack([jnp.stack([jnp.einsum('bhwc,bhwo->co', up[:, a:a + th, b:b + t...  38.5 us
    conv_general_dilated x14, local copies, waits for them, and re-layouts, _conv(): lax.conv_general_dilated(up, w, (1, 1), 'VALID', dimension_numbers=DN, pr...  35.9 us
    ppermute x8, starting transfers between devices, _edge(): prev = lax.ppermute(hi, name, [(i, i + 1) for i in range(n - 1)])  34.4 us
    psum x1, blocking collectives, body(): s = lax.psum(s.reshape(2, nb, GROUPS, cg).sum(-1), ('h', 'w')) / cnt  33.6 us
  transfers between devices with their start and end apart: 17, of which 1 were waited for; matrix products, arithmetic and copies ran while one was open for 35% of the time, Pallas kernels for 0%

commit v1 on v0

v1 whole, which is shorter than its diff:
```python
import jax
import jax.numpy as jnp
from jax import lax
from jax.experimental import pallas as pl
from jax.experimental.pallas import tpu as pltpu
from jax.sharding import PartitionSpec as P

GROUPS = 32
EPS = 1e-5
MESH = pl.DeviceIdType.MESH
F32 = jnp.float32
BF = jnp.bfloat16
ANY = pl.BlockSpec(memory_space=pl.ANY)
VM = pl.BlockSpec(memory_space=pltpu.VMEM)
TH, TW, C = 8, 256, 640
PIX = TH * TW
GC = 0.7978845608028654
GA = 0.044715


def _gelu_parts(n):
    n2 = n * n
    t = jnp.tanh(GC * n * (1.0 + GA * n2))
    return n2, t


def _halo_scratch():
    return [pltpu.VMEM((16, C), BF), pltpu.VMEM((3, 16, C), BF), pltpu.VMEM((2, TW, C), BF), pltpu.VMEM((16, C), F32), pltpu.VMEM((10, 8, C), F32),
            pltpu.SemaphoreType.DMA((5,)), pltpu.SemaphoreType.DMA((5,))]


class _Halo:
    def __init__(self, src, scratch):
        self.src = src
        self.edge, self.cols, self.rows, self.colf, self.colp, self.ssem, self.rsem = scratch
        self.w, self.h = lax.axis_index('w'), lax.axis_index('h')

    def _copy(self, i, a, b, dev):
        return pltpu.make_async_remote_copy(src_ref=a, dst_ref=b, send_sem=self.ssem.at[i], recv_sem=self.rsem.at[i], device_id=dev, device_id_type=MESH)

    def _copies(self):
        w, h = self.w, self.h
        return (self._copy(0, self.edge, self.cols.at[1], (1 - w, h)),
                self._copy(1, self.edge, self.cols.at[0], (1 - w, h + 1)),
                self._copy(2, self.edge, self.cols.at[2], (1 - w, h - 1)),
                self._copy(3, self.src.at[pl.ds(PIX - TW, TW)], self.rows.at[0], (w, h + 1)),
                self._copy(4, self.src.at[pl.ds(0, TW)], self.rows.at[1], (w, h - 1)))

    def start(self, nh=8):
        w, h = self.w, self.h
        c = self._copies()

        @pl.when(h < nh - 1)
        def _():
            c[3].start()

        @pl.when(h > 0)
        def _():
            c[4].start()
        for i in range(TH):
            first = self.src[i * TW:i * TW + 16, :].astype(F32)[0:1]
            last = self.src[i * TW + TW - 16:i * TW + TW, :].astype(F32)[15:16]
            self.colf[i:i + 1, :] = jnp.where(w == 0, last, first)
        self.colf[8:16, :] = jnp.zeros((8, C), F32)
        self.edge[...] = self.colf[...].astype(BF)
        c[0].start()

        @pl.when(h < nh - 1)
        def _():
            c[1].start()

        @pl.when(h > 0)
        def _():
            c[2].start()

        @pl.when(h == 0)
        def _():
            self.rows[0] = jnp.zeros((TW, C), BF)
            self.cols[0] = jnp.zeros((16, C), BF)

        @pl.when(h == nh - 1)
        def _():
            self.rows[1] = jnp.zeros((TW, C), BF)
            self.cols[2] = jnp.zeros((16, C), BF)

    def wait_cols(self, nh=8):
        h = self.h
        c = self._copies()
        c[0].wait()

        @pl.when(h < nh - 1)
        def _():
            c[1].wait_send()
            c[2].wait_recv()

        @pl.when(h > 0)
        def _():
            c[2].wait_send()
            c[1].wait_recv()
        self.colp[0, 0:1, :] = self.cols[0].astype(F32)[7:8]
        mine = self.cols[1].astype(F32)
        for i in range(TH):
            self.colp[i + 1, 0:1, :] = mine[i:i + 1]
        self.colp[9, 0:1, :] = self.cols[2].astype(F32)[0:1]

    def wait_rows(self, nh=8):
        h = self.h
        c = self._copies()

        @pl.when(h < nh - 1)
        def _():
            c[3].wait_send()
            c[4].wait_recv()

        @pl.when(h > 0)
        def _():
            c[4].wait_send()
            c[3].wait_recv()

    def row(self, cat, r, load):
        w = self.w
        ids = lax.broadcasted_iota(jnp.int32, (TW, 128), 0)
        out = pl.ds(r * TW if isinstance(r, int) else pl.multiple_of(r * TW, TW), TW)
        for k in range(C // 128):
            s = slice(k * 128, k * 128 + 128)
            x = load(s)
            xf = x.astype(F32)
            p = self.colp[r, 0:1, s]
            pl_ = jnp.where(w == 1, p, 0.0)
            pr = jnp.where(w == 0, p, 0.0)
            cat[out, s] = jnp.where(ids == 0, pl_, pltpu.roll(xf, 1, 0)).astype(BF)
            cat[out, C + k * 128:C + k * 128 + 128] = x
            cat[out, 2 * C + k * 128:2 * C + k * 128 + 128] = jnp.where(ids == TW - 1, pr, pltpu.roll(xf, TW - 1, 0)).astype(BF)

    def center(self, cat, r):
        o = pl.multiple_of((r - 1) * TW, TW)
        self.row(cat, r, lambda s: self.src[pl.ds(o, TW), s])

    def borders(self, cat):
        self.row(cat, 0, lambda s: self.rows[0, :, s])
        self.row(cat, TH + 1, lambda s: self.rows[1, :, s])


def _exchange(buf, ssem, rsem, rows, nh=8, nw=2):
    w, h = lax.axis_index('w'), lax.axis_index('h')
    me = w * nh + h
    n = nh * nw
    copies = []
    for d in range(1, n):
        to = lax.rem(me + d, n)
        copies.append(pltpu.make_async_remote_copy(
            src_ref=buf.at[0], dst_ref=buf.at[d], send_sem=ssem.at[d], recv_sem=rsem.at[d],
            device_id=(to // nh, lax.rem(to, nh)), device_id_type=MESH))
    for c in copies:
        c.start()
    return copies


def _exchange_sum(buf, copies, nh=8, nw=2):
    w, h = lax.axis_index('w'), lax.axis_index('h')
    me = w * nh + h
    n = nh * nw
    for c in copies:
        c.wait()
    total = None
    for src in range(n):
        v = buf[lax.rem(me - src + n, n)]
        total = v if total is None else total + v
    return total


def _group_mats():
    cg = C // GROUPS
    ch = lax.broadcasted_iota(jnp.int32, (C, 128), 0)
    gr = lax.broadcasted_iota(jnp.int32, (C, 128), 1) * cg
    down = jnp.where((ch >= gr) & (ch < gr + cg), 1.0, 0.0).astype(F32)
    ch = lax.broadcasted_iota(jnp.int32, (128, C), 1)
    gr = lax.broadcasted_iota(jnp.int32, (128, C), 0) * cg
    up = jnp.where((ch >= gr) & (ch < gr + cg), 1.0, 0.0).astype(F32)
    return down, up


def _dotf(a, b):
    return jnp.dot(a, b, preferred_element_type=F32, precision=lax.Precision.HIGHEST)


def _conv(cat, w, m0, mb):
    acc = None
    for a in range(3):
        d = jnp.dot(cat[pl.ds(pl.multiple_of(m0 + a * TW, TW), mb), :], w[a], preferred_element_type=F32)
        acc = d if acc is None else acc + d
    return acc


def _conv_t(cat, w, m0, mb):
    acc = None
    for a in range(3):
        rows = pl.ds(pl.multiple_of(m0 + a * TW, TW), mb)
        for b in range(3):
            d = lax.dot_general(cat[rows, b * C:b * C + C], w[2 - a, (2 - b) * C:(2 - b) * C + C, :],
                                (((1,), (1,)), ((), ())), preferred_element_type=F32)
            acc = d if acc is None else acc + d
    return acc


def _k1(cnt, x, w1, g, gamma, beta, gcat_o, a_o, z_o, zt_o, stat_o,
        xv, gv, wv, cat, gcat, av, zv, ztv, sums, ebuf, ess, ers, dsem, *hs):
    n = len(hs) // 2
    hx, hg = _Halo(xv, hs[:n]), _Halo(gv, hs[n:])
    cx = pltpu.make_async_copy(x, xv, dsem.at[0])
    cg_ = pltpu.make_async_copy(g, gv, dsem.at[1])
    cw = pltpu.make_async_copy(w1, wv, dsem.at[2])
    cx.start()
    cg_.start()
    cw.start()
    cx.wait()
    hx.start()
    cg_.wait()
    hg.start()
    sums[...] = jnp.zeros_like(sums)
    hx.wait_cols()

    @pl.loop(1, TH + 1)
    def _(r):
        hx.center(cat, r)
    hx.wait_rows()
    hx.borders(cat)
    hg.wait_cols()
    cw.wait()

    @pl.loop(0, 4)
    def _(i):
        m0 = pl.multiple_of(i * 512, 512)
        a = _conv(cat, wv, m0, 512).astype(BF)
        av[pl.ds(m0, 512), :] = a
        af = a.astype(F32)
        sums[0:1, :] += jnp.sum(af, axis=0, keepdims=True)
        sums[1:2, :] += jnp.sum(af * af, axis=0, keepdims=True)
        hg.center(gcat, 2 * i + 1)
        hg.center(gcat, 2 * i + 2)
    ca = pltpu.make_async_copy(av, a_o, dsem.at[3])
    ca.start()
    down, up = _group_mats()
    ebuf[0] = _dotf(sums[...], down)
    copies = _exchange(ebuf, ess, ers, 8)
    hg.wait_rows()
    hg.borders(gcat)
    cgo = pltpu.make_async_copy(gcat, gcat_o, dsem.at[4])
    cgo.start()
    tot = _exchange_sum(ebuf, copies) * (1.0 / cnt)
    mean_g = tot[0:1]
    rstd_g = lax.rsqrt(tot[1:2] - mean_g * mean_g + EPS)
    row = lax.broadcasted_iota(jnp.int32, (8, 128), 0)
    st = jnp.where(row == 0, mean_g, jnp.where(row == 1, rstd_g, 0.0))
    st = _dotf(st, up)
    stat_o[...] = st
    sums[...] = st

    @pl.loop(0, 8)
    def _(i):
        m0 = pl.multiple_of(i * TW, TW)
        for k in range(C // 128):
            s = slice(k * 128, k * 128 + 128)
            xh = (av[pl.ds(m0, TW), s].astype(F32) - sums[0:1, s]) * sums[1:2, s]
            nn = xh * gamma[:, s] + beta[:, s]
            _, t = _gelu_parts(nn)
            z = nn * (0.5 * (1.0 + t))
            zv[pl.ds(m0, TW), s] = z.astype(BF)
            ztv[s, pl.ds(m0, TW)] = z.T.astype(BF)
    cz = pltpu.make_async_copy(zv, z_o, dsem.at[5])
    czt = pltpu.make_async_copy(ztv, zt_o, dsem.at[6])
    cz.start()
    czt.start()
    ca.wait()
    cgo.wait()
    cz.wait()
    czt.wait()


def _wgrad_block(lt, cat, a, c0):
    rows = pl.ds(pl.multiple_of(c0, 32), 160)
    return jnp.dot(lt[rows, :], cat[pl.ds(pl.multiple_of((2 - a) * TW, TW), PIX), :], preferred_element_type=F32)


def _k2(cnt, gcat_i, zt_i, a_i, stat, gamma, beta, w2, dw_o, da_o, t_o,
        cat, lt, av, wv, dn, blk, sums, ebuf, ess, ers, dsem, bsem):
    ins = [pltpu.make_async_copy(s, d, dsem.at[i]) for i, (s, d) in enumerate(((zt_i, lt), (gcat_i, cat), (w2, wv), (a_i, av)))]
    for c in ins:
        c.start()
    sums[...] = jnp.zeros_like(sums)
    ins[0].wait()
    ins[1].wait()

    def out(j, slot):
        a, q = j // 4, lax.rem(j, 4)
        return pltpu.make_async_copy(blk.at[slot], dw_o.at[a, :, pl.ds(pl.multiple_of(q * 160, 32), 160), :], bsem.at[slot])

    @pl.loop(0, 12)
    def _(j):
        a, q = j // 4, lax.rem(j, 4)
        slot = lax.rem(j, 2)

        @pl.when(j >= 2)
        def _():
            out(j - 2, slot).wait()
        acc = _wgrad_block(lt, cat, a, q * 160)
        for b in range(3):
            blk[slot, b] = acc[:, (2 - b) * C:(2 - b) * C + C]
        out(j, slot).start()
    ins[2].wait()
    ins[3].wait()

    @pl.loop(0, 4)
    def _(i):
        m0 = pl.multiple_of(i * 512, 512)
        dz = _conv_t(cat, wv, m0, 512)
        xh = (av[pl.ds(m0, 512), :].astype(F32) - stat[0:1, :]) * stat[1:2, :]
        nn = xh * gamma[...] + beta[...]
        n2, t = _gelu_parts(nn)
        d = dz * (0.5 * (1.0 + t) + (0.5 * GC) * nn * (1.0 - t * t) * (1.0 + (3.0 * GA) * n2))
        dn[pl.ds(m0, 512), :] = d
        sums[0:1, :] += jnp.sum(d * xh, axis=0, keepdims=True)
        sums[1:2, :] += jnp.sum(d, axis=0, keepdims=True)
    for s in range(2):
        for k in range(5):
            ebuf[0, s * 8 + k:s * 8 + k + 1, :] = sums[s:s + 1, k * 128:k * 128 + 128]
        ebuf[0, s * 8 + 5:s * 8 + 8, :] = jnp.zeros((3, 128), F32)
    copies = _exchange(ebuf, ess, ers, 16)
    out(10, 0).wait()
    out(11, 1).wait()
    tot = _exchange_sum(ebuf, copies)
    for s in range(2):
        for k in range(5):
            sums[s:s + 1, k * 128:k * 128 + 128] = tot[s * 8 + k:s * 8 + k + 1, :]
    t_o[...] = sums[...]
    down, up = _group_mats()
    u = _dotf(_dotf(sums[...] * gamma[...], down) * (1.0 / cnt), up)
    sums[...] = u

    @pl.loop(0, 8)
    def _(i):
        m = pl.ds(pl.multiple_of(i * TW, TW), TW)
        for k in range(C // 128):
            s = slice(k * 128, k * 128 + 128)
            xh = (av[m, s].astype(F32) - stat[0:1, s]) * stat[1:2, s]
            v = stat[1:2, s] * (dn[m, s] * gamma[:, s] - sums[1:2, s] - xh * sums[0:1, s])
            av[m, s] = v.astype(BF)
    co = pltpu.make_async_copy(av, da_o, dsem.at[0])
    co.start()
    co.wait()


def _k3(x, z, da, g, w1, w2, dw_o, y_o, dx_o, xv, zv, dav, gv, lt, wv, w2v, cat, blk, ob, dsem, bsem, *hs):
    n = len(hs) // 2
    hd, hz = _Halo(dav, hs[:n]), _Halo(zv, hs[n:])
    ins = [pltpu.make_async_copy(s, d, dsem.at[i]) for i, (s, d) in enumerate(((da, dav), (x, xv), (z, zv), (w1, wv), (g, gv), (w2, w2v)))]
    for c in ins:
        c.start()
    ins[0].wait()
    hd.start()
    ins[2].wait()
    hz.start()
    ins[1].wait()

    @pl.loop(0, 8)
    def _(i):
        m = pl.ds(pl.multiple_of(i * TW, TW), TW)
        for k in range(C // 128):
            s = slice(k * 128, k * 128 + 128)
            lt[s, m] = xv[m, s].astype(F32).T.astype(BF)
    hd.wait_cols()

    @pl.loop(1, TH + 1)
    def _(r):
        hd.center(cat, r)
    hd.wait_rows()
    hd.borders(cat)

    def out(j, slot):
        a, q = j // 4, lax.rem(j, 4)
        return pltpu.make_async_copy(blk.at[slot], dw_o.at[a, :, pl.ds(pl.multiple_of(q * 160, 32), 160), :], bsem.at[slot])

    @pl.loop(0, 12)
    def _(j):
        a, q = j // 4, lax.rem(j, 4)
        slot = lax.rem(j, 2)

        @pl.when(j >= 2)
        def _():
            out(j - 2, slot).wait()
        acc = _wgrad_block(lt, cat, a, q * 160)
        for b in range(3):
            blk[slot, b] = acc[:, (2 - b) * C:(2 - b) * C + C]
        out(j, slot).start()
    out(10, 0).wait()
    out(11, 1).wait()
    ins[3].wait()
    ins[4].wait()

    @pl.loop(0, 4)
    def _(i):
        m = pl.ds(pl.multiple_of(i * 512, 512), 512)
        ob[m, :] = (_conv_t(cat, wv, i * 512, 512) + gv[m, :].astype(F32)).astype(BF)
    c1 = pltpu.make_async_copy(ob, dx_o, dsem.at[0])
    c1.start()
    hz.wait_cols()

    @pl.loop(1, TH + 1)
    def _(r):
        hz.center(cat, r)
    hz.wait_rows()
    hz.borders(cat)
    ins[5].wait()
    c1.wait()

    @pl.loop(0, 4)
    def _(i):
        m = pl.ds(pl.multiple_of(i * 512, 512), 512)
        ob[m, :] = (_conv(cat, w2v, i * 512, 512) + xv[m, :].astype(F32)).astype(BF)
    c2 = pltpu.make_async_copy(ob, y_o, dsem.at[1])
    c2.start()
    c2.wait()


def _params(**kw):
    return pltpu.CompilerParams(has_side_effects=True, vmem_limit_bytes=64 * 2**20 - 65536, **kw)


def solution(mesh):
    tile = P(None, 'h', 'w', None)
    cnt = float(TH * TW * 16 * (C // GROUPS))
    sds = jax.ShapeDtypeStruct
    DMA = pltpu.SemaphoreType.DMA
    V = pltpu.VMEM

    def body(x, w1, gamma, beta, w2, g):
        x2, g2 = x.reshape(PIX, C), g.reshape(PIX, C)
        w1r, w2r = w1.reshape(3, 3 * C, C), w2.reshape(3, 3 * C, C)
        ga, be = gamma.reshape(1, C), beta.reshape(1, C)
        gcat, a, z, zt, stat = pl.pallas_call(
            lambda *r: _k1(cnt, *r),
            out_shape=[sds((10 * TW, 3 * C), BF), sds((PIX, C), BF), sds((PIX, C), BF), sds((C, PIX), BF), sds((8, C), F32)],
            in_specs=[ANY, ANY, ANY, VM, VM], out_specs=[ANY, ANY, ANY, ANY, VM],
            scratch_shapes=[V((PIX, C), BF), V((PIX, C), BF), V((3, 3 * C, C), BF), V((10 * TW, 3 * C), BF), V((10 * TW, 3 * C), BF),
                            V((PIX, C), BF), V((PIX, C), BF), V((C, PIX), BF), V((8, C), F32), V((16, 8, 128), F32), DMA((16,)), DMA((16,)), DMA((8,))]
            + _halo_scratch() + _halo_scratch(),
            compiler_params=_params(), name='k1')(x2, w1r, g2, ga, be)
        dw2p, da, t = pl.pallas_call(
            lambda *r: _k2(cnt, *r),
            out_shape=[sds((3, 3, C, C), F32), sds((PIX, C), BF), sds((8, C), F32)],
            in_specs=[ANY, ANY, ANY, VM, VM, VM, ANY], out_specs=[ANY, ANY, VM],
            scratch_shapes=[V((10 * TW, 3 * C), BF), V((C, PIX), BF), V((PIX, C), BF), V((3, 3 * C, C), BF), V((PIX, C), F32),
                            V((2, 3, 160, C), F32), V((8, C), F32), V((16, 16, 128), F32), DMA((16,)), DMA((16,)), DMA((8,)), DMA((2,))],
            compiler_params=_params(), name='k2')(gcat, zt, a, stat, ga, be, w2r)
        dw1p, y, dx = pl.pallas_call(
            _k3,
            out_shape=[sds((3, 3, C, C), F32), sds((PIX, C), BF), sds((PIX, C), BF)],
            in_specs=[ANY] * 6, out_specs=[ANY, ANY, ANY],
            scratch_shapes=[V((PIX, C), BF)] * 4 + [V((C, PIX), BF), V((3, 3 * C, C), BF), V((3, 3 * C, C), BF), V((10 * TW, 3 * C), BF),
                            V((2, 3, 160, C), F32), V((PIX, C), BF), DMA((8,)), DMA((2,))]
            + _halo_scratch() + _halo_scratch(),
            compiler_params=_params(), name='k3')(x2, z, da, g2, w1r, w2r)
        dw2 = lax.psum(dw2p, ('h', 'w'))
        dw1 = lax.psum(dw1p, ('h', 'w'))
        return y.reshape(x.shape), dx.reshape(x.shape), dw1, dw2, t[0], t[1]

    return jax.shard_map(body, mesh=mesh, in_specs=(tile, P(), P(), P(), P(), tile), out_specs=(tile, tile, P(), P(), P(), P()), check_vma=False)
```

time: 708 us -> 525 us (0.74); the launches traced: 700 us -> 524 us
  Pallas kernels: 0 us -> 191 us
  matrix products: 172 us -> 0 us
  waiting for transfers between devices: 157 us -> 287 us
  local copies, waits for them, and re-layouts: 161 us -> 31.5 us
  other arithmetic: 82.4 us -> 0 us
  blocking collectives: 66.6 us -> 0 us
  starting transfers between devices: 44.7 us -> 0.04 us
    pallas_call x0 -> x3, Pallas kernels: none -> 191 us  [the longest x1 73.2 us: body(): pl.pallas_call(_k3, out_shape=[sds((3, 3, C, C), F32), sds((PIX, C), BF),...]
    psum x1, waiting for transfers between devices: 157 us -> 287 us  [body(): dw1 = lax.psum(dw1p, ('h', 'w'))]
    conv_general_dilated x4 -> x0, matrix products: 113 us -> none  [_conv(): lax.conv_general_dilated(up, w, (1, 1), 'VALID', dimension_numbers=DN, pr...]
    psum x2 -> x0, blocking collectives: 66.6 us -> none  [the longest x1 33.6 us: body(): s = lax.psum(s.reshape(2, nb, GROUPS, cg).sum(-1), ('h', 'w')) / cnt]
    dot_general x18 -> x0, matrix products: 59.3 us -> none  [_wgrad(): jnp.einsum('bhwc,bhwo->co', up[:, a:a + th, b:b + tw], v, preferred_eleme...]
    ppermute x16 -> x0, starting transfers between devices: 44.7 us -> none  [the longest x8 34.4 us: _edge(): prev = lax.ppermute(hi, name, [(i, i + 1) for i in range(n - 1)])]
    unnamed x75 -> x8, local copies, waits for them, and re-layouts: 67.4 us -> 27.5 us
    another operation x8 -> x0, other arithmetic: 38.5 us -> none  [the longest x7 38.5 us: _wgrad(): jnp.stack([jnp.stack([jnp.einsum('bhwc,bhwo->co', up[:, a:a + th, b:b + t...]
  transfers between devices with their start and end apart: 17 -> 1, of which waited for: 1 -> 1; matrix products, arithmetic and copies ran while one was open for 35% -> 0% of each run, Pallas kernels for 0% -> 0%
where the time goes in v1:
time: 525 us; the launch traced here: 524 us
  waiting for transfers between devices  287 us (55%)
  Pallas kernels  191 us (36%)
  local copies, waits for them, and re-layouts  31.5 us (6%)
  between operations  14.1 us (3%)
    psum x1, waiting for transfers between devices, body(): dw1 = lax.psum(dw1p, ('h', 'w'))  287 us
    pallas_call x1, Pallas kernels, body(): pl.pallas_call(_k3, out_shape=[sds((3, 3, C, C), F32), sds((PIX, C), BF),...  73.2 us
    pallas_call x1, Pallas kernels, body(): pl.pallas_call(lambda *r: _k2(cnt, *r), out_shape=[sds((3, 3, C, C), F32)...  60.6 us
    pallas_call x1, Pallas kernels, body(): pl.pallas_call(lambda *r: _k1(cnt, *r), out_shape=[sds((10 * TW, 3 * C),...  57.6 us
    unnamed x8, local copies, waits for them, and re-layouts  27.5 us
  transfers between devices with their start and end apart: 1, of which 1 were waited for; matrix products, arithmetic and copies ran while one was open for 0% of the time, Pallas kernels for 0%

profile of v1, /device:TPU:0, one launch (start us, length us, event | category | flops | bytes accessed | tf_op | source)
XLA Modules:
  0.0 524.2 jit_solution(7794945871348186836)
XLA Ops:
  7.2 0.0 all-reduce.3.cloned.1.call-start
  7.2 1.3 reshape.39.r_3_.r_4_
  8.5 1.3 reshape.40.r_4_.r_5_
  9.7 57.6 %k1.1 = (bf16[2560,1920]{1,0:T(8,128)(2,1)}, bf16[2048,640]{1,0:T(8,128)(2,1)}, bf16[2048,640]{1,0:T(8,128)(2,1)}, bf16[640,2048]{1,0:T(8,128)(2,1)}, f32[8,640]{1,0:T(8,128)}) custom-call(bf16[2048,640]{1,0:T(8,128)(2,1)} %bitcast.10, bf16[3,1920,640]{2,1,0:T(8,128)(2,1)} %bitcast.6, bf16[2048,640]{1,0:T(8,128)(2,1)} %bitcast.12, ...), custom_call_target="tpu_custom_call" | custom-call | tf_op jit(solution)/shard_map/k1/pallas_call | solution.py:440
  67.4 60.6 %k2.1 = (f32[3,3,640,640]{3,2,1,0:T(8,128)}, bf16[2048,640]{1,0:T(8,128)(2,1)}, f32[8,640]{1,0:T(8,128)}) custom-call(bf16[2560,1920]{1,0:T(8,128)(2,1)} %get-tuple-element.18.r_0_, bf16[640,2048]{1,0:T(8,128)(2,1)} %get-tuple-element.19.r_1_, bf16[2048,640]{1,0:T(8,128)(2,1)} %get-tuple-element.20.r_2_, f32[8,640]{1,0:T(8,128)} %get-tuple-element.21.r_3_, ...), custom_call_target="tpu_custom_call" | custom-call | tf_op jit(solution)/shard_map/k2/pallas_call | solution.py:448
  128.0 73.2 %k3.1 = (f32[3,3,640,640]{3,2,1,0:T(8,128)}, bf16[2048,640]{1,0:T(8,128)(2,1)}, bf16[2048,640]{1,0:T(8,128)(2,1)}) custom-call(bf16[2048,640]{1,0:T(8,128)(2,1)} %bitcast.11, bf16[2048,640]{1,0:T(8,128)(2,1)} %get-tuple-element.17.z, bf16[2048,640]{1,0:T(8,128)(2,1)} %get-tuple-element.22.da, bf16[2048,640]{1,0:T(8,128)(2,1)} %bitcast.13, ...), custom_call_target="tpu_custom_call" | custom-call | tf_op jit(solution)/shard_map/k3/pallas_call | solution.py:455
  201.2 0.0 copy-start.1
  201.3 0.0 all-reduce.3.cloned.1.call-update
  201.3 1.5 slice_reduce_fusion
  202.8 287.1 %all-reduce.3.cloned.1.call-done = (f32[3,3,640,640]{3,2,1,0:T(8,128)}, f32[3,3,640,640]{3,2,1,0:T(8,128)}) async-done(((f32[3,3,640,640]{3,2,1,0:T(8,128)}, f32[3,3,640,640]{3,2,1,0:T(8,128)}), (f32[3,3,640,640]{3,2,1,0:T(8,128)}, f32[3,3,640,640]{3,2,1,0:T(8,128)})) %all-reduce.3.cloned.1.call-update) | async-done | bytes 29491216 | tf_op jit(solution)/shard_map/psum | solution.py:464
  489.9 0.0 copy-done.1
  489.9 0.0 copy-start
  489.9 1.5 copy.18
  491.4 1.2 copy-done
  492.6 1.5 copy.19
  494.1 11.6 %copy.20 = f32[3,3,640,640]{3,2,1,0:T(8,128)} copy(f32[3,3,640,640]{3,2,1,0:T(8,128)} %get-tuple-element.40) | data formatting | bytes 29491200
  505.7 11.6 %copy.21 = f32[3,3,640,640]{3,2,1,0:T(8,128)} copy(f32[3,3,640,640]{3,2,1,0:T(8,128)} %get-tuple-element.41) | data formatting | bytes 29491200
Async XLA Ops:
  7.2 482.7 %all-reduce.3.cloned.1.call-start = ((), (), s32[]{:S(2)}) async-start(), calls=%async_computation | async-start | bytes 58982400 | tf_op jit(solution)/shard_map/psum | solution.py:464
  201.2 288.7 %copy-start.1 = (bf16[2048,640]{1,0:T(8,128)(2,1)S(1)}, bf16[2048,640]{1,0:T(8,128)(2,1)}, u32[]{:S(2)}) copy-start(bf16[2048,640]{1,0:T(8,128)(2,1)} %get-tuple-element.23) | copy-start | bytes 7864324
  489.9 2.7 copy-start
Sparse Core Ops, SparseCore 0:
  201.4 288.4 all-reduce.2

commit v2 on v1

v2 whole, which is shorter than its diff:
```python
import jax
import jax.numpy as jnp
from jax import lax
from jax.experimental import pallas as pl
from jax.experimental.pallas import tpu as pltpu
from jax.sharding import PartitionSpec as P

GROUPS = 32
EPS = 1e-5
MESH = pl.DeviceIdType.MESH
F32 = jnp.float32
BF = jnp.bfloat16
ANY = pl.BlockSpec(memory_space=pl.ANY)
VM = pl.BlockSpec(memory_space=pltpu.VMEM)
TH, TW, C = 8, 256, 640
PIX = TH * TW
GC = 0.7978845608028654
GA = 0.044715


T3 = (0, 1, 2)
KB = tuple((k, b) for k in T3 for b in T3)
LANES = tuple(slice(k, k + 128) for k in range(0, C, 128))


def _mul(v, m):
    return pl.multiple_of(v, m)


def _rows(i, n):
    return pl.ds(_mul(i * n, n), n)


def _tiles(f):
    @pl.loop(0, TH)
    def _(i):
        for s in LANES:
            f(_rows(i, TW), s)


def _blocks(f):
    @pl.loop(0, 4)
    def _(i):
        f(i, _mul(i * 512, 512), _rows(i, 512))


def _load(pairs, sem):
    copies = [pltpu.make_async_copy(a, b, sem.at[i]) for i, (a, b) in enumerate(pairs)]
    for c in copies:
        c.start()
    return copies


def _gelu_parts(n):
    n2 = n * n
    t = jnp.tanh(GC * n * (1.0 + GA * n2))
    return n2, t


def _halo_scratch():
    return [pltpu.VMEM((16, C), BF), pltpu.VMEM((3, 16, C), BF), pltpu.VMEM((2, TW, C), BF), pltpu.VMEM((16, C), F32), pltpu.VMEM((10, 8, C), F32),
            pltpu.SemaphoreType.DMA((5,)), pltpu.SemaphoreType.DMA((5,))]


class _Halo:
    def __init__(self, src, scratch):
        self.src = src
        self.edge, self.cols, self.rows, self.colf, self.colp, self.ssem, self.rsem = scratch
        self.w, self.h = lax.axis_index('w'), lax.axis_index('h')

    def _copy(self, i, a, b, dev):
        return pltpu.make_async_remote_copy(src_ref=a, dst_ref=b, send_sem=self.ssem.at[i], recv_sem=self.rsem.at[i], device_id=dev, device_id_type=MESH)

    def _copies(self):
        w, h = self.w, self.h
        return (self._copy(0, self.edge, self.cols.at[1], (1 - w, h)),
                self._copy(1, self.edge, self.cols.at[0], (1 - w, h + 1)),
                self._copy(2, self.edge, self.cols.at[2], (1 - w, h - 1)),
                self._copy(3, self.src.at[pl.ds(PIX - TW, TW)], self.rows.at[0], (w, h + 1)),
                self._copy(4, self.src.at[pl.ds(0, TW)], self.rows.at[1], (w, h - 1)))

    def start(self, nh=8):
        w, h = self.w, self.h
        c = self._copies()

        @pl.when(h < nh - 1)
        def _():
            c[3].start()

        @pl.when(h > 0)
        def _():
            c[4].start()
        for i in range(TH):
            first = self.src[i * TW:i * TW + 16, :].astype(F32)[0:1]
            last = self.src[i * TW + TW - 16:i * TW + TW, :].astype(F32)[15:16]
            self.colf[i:i + 1, :] = jnp.where(w == 0, last, first)
        self.colf[8:16, :] = jnp.zeros((8, C), F32)
        self.edge[...] = self.colf[...].astype(BF)
        c[0].start()

        @pl.when(h < nh - 1)
        def _():
            c[1].start()

        @pl.when(h > 0)
        def _():
            c[2].start()

        @pl.when(h == 0)
        def _():
            self.rows[0] = jnp.zeros((TW, C), BF)
            self.cols[0] = jnp.zeros((16, C), BF)

        @pl.when(h == nh - 1)
        def _():
            self.rows[1] = jnp.zeros((TW, C), BF)
            self.cols[2] = jnp.zeros((16, C), BF)

    def wait_cols(self, nh=8):
        h = self.h
        c = self._copies()
        c[0].wait()

        @pl.when(h < nh - 1)
        def _():
            c[1].wait_send()
            c[2].wait_recv()

        @pl.when(h > 0)
        def _():
            c[2].wait_send()
            c[1].wait_recv()
        self.colp[0, 0:1, :] = self.cols[0].astype(F32)[7:8]
        mine = self.cols[1].astype(F32)
        for i in range(TH):
            self.colp[i + 1, 0:1, :] = mine[i:i + 1]
        self.colp[9, 0:1, :] = self.cols[2].astype(F32)[0:1]

    def wait_rows(self, nh=8):
        h = self.h
        c = self._copies()

        @pl.when(h < nh - 1)
        def _():
            c[3].wait_send()
            c[4].wait_recv()

        @pl.when(h > 0)
        def _():
            c[4].wait_send()
            c[3].wait_recv()

    def row(self, cat, r, load):
        w = self.w
        ids = lax.broadcasted_iota(jnp.int32, (TW, 128), 0)
        out = pl.ds(r * TW if isinstance(r, int) else pl.multiple_of(r * TW, TW), TW)
        for s in LANES:
            k = s.start
            x = load(s)
            xf = x.astype(F32)
            p = self.colp[r, 0:1, s]
            pl_ = jnp.where(w == 1, p, 0.0)
            pr = jnp.where(w == 0, p, 0.0)
            cat[out, s] = jnp.where(ids == 0, pl_, pltpu.roll(xf, 1, 0)).astype(BF)
            cat[out, C + k:C + k + 128] = x
            cat[out, 2 * C + k:2 * C + k + 128] = jnp.where(ids == TW - 1, pr, pltpu.roll(xf, TW - 1, 0)).astype(BF)

    def center(self, cat, r):
        o = pl.multiple_of((r - 1) * TW, TW)
        self.row(cat, r, lambda s: self.src[pl.ds(o, TW), s])

    def centers(self, cat):
        @pl.loop(1, TH + 1)
        def _(r):
            self.center(cat, r)

    def borders(self, cat):
        self.row(cat, 0, lambda s: self.rows[0, :, s])
        self.row(cat, TH + 1, lambda s: self.rows[1, :, s])


def _exchange(buf, ssem, rsem, nh=8, nw=2):
    w, h = lax.axis_index('w'), lax.axis_index('h')
    me = w * nh + h
    n = nh * nw
    copies = []
    for d in range(1, n):
        to = lax.rem(me + d, n)
        copies.append(pltpu.make_async_remote_copy(
            src_ref=buf.at[0], dst_ref=buf.at[d], send_sem=ssem.at[d], recv_sem=rsem.at[d],
            device_id=(to // nh, lax.rem(to, nh)), device_id_type=MESH))
    for c in copies:
        c.start()
    return copies


def _exchange_sum(buf, copies, nh=8, nw=2):
    w, h = lax.axis_index('w'), lax.axis_index('h')
    me = w * nh + h
    n = nh * nw
    for c in copies:
        c.wait()
    total = None
    for src in range(n):
        v = buf[lax.rem(me - src + n, n)]
        total = v if total is None else total + v
    return total


def _group_mats():
    cg = C // GROUPS
    ch = lax.broadcasted_iota(jnp.int32, (C, 128), 0)
    gr = lax.broadcasted_iota(jnp.int32, (C, 128), 1) * cg
    down = jnp.where((ch >= gr) & (ch < gr + cg), 1.0, 0.0).astype(F32)
    ch = lax.broadcasted_iota(jnp.int32, (128, C), 1)
    gr = lax.broadcasted_iota(jnp.int32, (128, C), 0) * cg
    up = jnp.where((ch >= gr) & (ch < gr + cg), 1.0, 0.0).astype(F32)
    return down, up


def _dotf(a, b):
    return jnp.dot(a, b, preferred_element_type=F32, precision=lax.Precision.HIGHEST)


def _conv(cat, w, m0, mb):
    acc = None
    for a in range(3):
        d = jnp.dot(cat[pl.ds(pl.multiple_of(m0 + a * TW, TW), mb), :], w[a], preferred_element_type=F32)
        acc = d if acc is None else acc + d
    return acc


def _conv_t(cat, w, m0, mb):
    acc = None
    for a in range(3):
        rows = pl.ds(pl.multiple_of(m0 + a * TW, TW), mb)
        for b in range(3):
            d = lax.dot_general(cat[rows, b * C:b * C + C], w[2 - a, (2 - b) * C:(2 - b) * C + C, :],
                                (((1,), (1,)), ((), ())), preferred_element_type=F32)
            acc = d if acc is None else acc + d
    return acc


def _k1(cnt, x, w1, g, gamma, beta, gcat_o, a_o, z_o, zt_o, xt_o, stat_o,
        xv, gv, wv, cat, gcat, av, zv, ztv, xtv, sums, ebuf, ess, ers, dsem, osem, *hs):
    n = len(hs) // 2
    hx, hg = _Halo(xv, hs[:n]), _Halo(gv, hs[n:])
    cx, cg, cw = _load(((x, xv), (g, gv), (w1, wv)), dsem)
    cx.wait()
    hx.start()
    cg.wait()
    hg.start()
    sums[...] = jnp.zeros_like(sums)
    hx.wait_cols()
    hx.centers(cat)
    hx.wait_rows()
    hx.borders(cat)
    hg.wait_cols()
    cw.wait()

    def conv(i, m0, m):
        a = _conv(cat, wv, m0, 512).astype(BF)
        av[m, :] = a
        af = a.astype(F32)
        sums[0:1, :] += jnp.sum(af, axis=0, keepdims=True)
        sums[1:2, :] += jnp.sum(af * af, axis=0, keepdims=True)
        for r in (2 * i, 2 * i + 1):
            hg.center(gcat, r + 1)
            for s in LANES:
                xtv[s, _rows(r, TW)] = xv[_rows(r, TW), s].astype(F32).T.astype(BF)
    _blocks(conv)
    down, up = _group_mats()
    ebuf[0] = _dotf(sums[...], down)
    copies = _exchange(ebuf, ess, ers)
    outs = _load(((av, a_o), (xtv, xt_o)), osem)
    hg.wait_rows()
    hg.borders(gcat)
    outs += _load(((gcat, gcat_o),), dsem)
    tot = _exchange_sum(ebuf, copies) * (1.0 / cnt)
    mean_g = tot[0:1]
    rstd_g = lax.rsqrt(tot[1:2] - mean_g * mean_g + EPS)
    row = lax.broadcasted_iota(jnp.int32, (8, 128), 0)
    st = jnp.where(row == 0, mean_g, jnp.where(row == 1, rstd_g, 0.0))
    st = _dotf(st, up)
    stat_o[...] = st
    sums[...] = st

    def act(m, s):
        nn = (av[m, s].astype(F32) - sums[0:1, s]) * sums[1:2, s] * gamma[:, s] + beta[:, s]
        _, t = _gelu_parts(nn)
        z = nn * (0.5 * (1.0 + t))
        zv[m, s] = z.astype(BF)
        ztv[s, m] = z.T.astype(BF)
    _tiles(act)
    outs += _load(((zv, z_o), (ztv, zt_o)), dsem.at[pl.ds(1, 2)])
    for c in outs:
        c.wait()


def _wgrad_block(lt, cat, a, c0):
    rows = pl.ds(pl.multiple_of(c0, 32), 160)
    return jnp.dot(lt[rows, :], cat[pl.ds(pl.multiple_of((2 - a) * TW, TW), PIX), :], preferred_element_type=F32)


class _Place:
    def __init__(self):
        self.w, self.h = lax.axis_index('w'), lax.axis_index('h')
        self.core = lax.rem(self.h, 2)
        self.chip = self.h // 2 + 4 * self.w

    def _axis(self, k):
        return 1 + k + k * (k - 1) // 2

    def bit(self, k):
        return lax.rem(self.chip // self._axis(k), 2)

    def across(self, k):
        chip = self.chip + self._axis(k) * (1 - 2 * self.bit(k))
        return chip // 4, lax.rem(chip, 4) * 2 + self.core

    def partner(self):
        return self.w, self.h + 1 - 2 * self.core


def _rcopy(src, dst, ss, rs, dev):
    return pltpu.make_async_remote_copy(src_ref=src, dst_ref=dst, send_sem=ss, recv_sem=rs, device_id=dev, device_id_type=MESH)


DMA = pltpu.SemaphoreType.DMA
Q, HALF, QUART, EIGHTH = 160, 480, 80, 40


def _rs_buffers():
    return [pltpu.VMEM((12 * HALF, C), F32), pltpu.VMEM((6, HALF, C), F32), pltpu.VMEM((3, HALF, C), F32)]


def _rs_scratch():
    return [pltpu.VMEM((3, 3, QUART, C), F32), pltpu.VMEM((3, 3, EIGHTH, C), F32)] + [DMA((6,))] * 2 + [DMA((3,))] * 2 + [DMA((3, 3))] * 4


class _Scatter:
    def __init__(self, place, bufs, own):
        self.pl = place
        self.p, self.d, self.r1 = bufs
        self.r2, self.r3, self.ds, self.dr, self.s1, self.q1, self.s2, self.q2, self.s3, self.q3 = own

    def _d2d(self, i):
        return _rcopy(self.p.at[_rows(i, HALF), :], self.d.at[i], self.ds.at[i], self.dr.at[i], self.pl.partner())

    def _rs1(self, k):
        return _rcopy(self.p.at[_rows(k + 6, HALF), :], self.r1.at[k], self.s1.at[k], self.q1.at[k], self.pl.across(k))

    def _half(self, k, d, n):
        return self.pl.bit((k + d) % 3) * n

    def _at(self, k, b, o, n):
        return pl.ds(_mul((k + 9) * HALF + b * Q + o, 8), n)

    def _rs2(self, k, b):
        src = self.p.at[self._at(k, b, QUART - self._half(k, 1, QUART), QUART), :]
        return _rcopy(src, self.r2.at[k, b], self.s2.at[k, b], self.q2.at[k, b], self.pl.across((k + 1) % 3))

    def _rs3(self, k, b):
        src = self.p.at[self._at(k, b, self._half(k, 1, QUART) + EIGHTH - self._half(k, 2, EIGHTH), EIGHTH), :]
        return _rcopy(src, self.r3.at[k, b], self.s3.at[k, b], self.q3.at[k, b], self.pl.across((k + 2) % 3))

    def block(self, j, lt, cat):
        me = self.pl
        phase, k = j // 3, lax.rem(j, 3)
        own, keep = lax.rem(phase, 2), phase // 2
        b1 = me.bit(k)
        core = me.core * own + (1 - me.core) * (1 - own)
        half = b1 * keep + (1 - b1) * (1 - keep)
        i = keep * 3 + k
        base = (own * 6 + i) * HALF
        acc = _wgrad_block(lt, cat, k, core * 2 * Q + half * Q)
        for b in T3:
            lo = (2 - b) * C
            self.p[pl.ds(_mul(base + b * Q, Q), Q), :] = acc[:, lo:lo + C]

        @pl.when(own == 0)
        def _():
            self._d2d(i).start()

        @pl.when(own == 1)
        def _():
            self._d2d(i).wait_recv()
            self.p[pl.ds(_mul(base, Q), HALF), :] += self.d[i]

        @pl.when(phase == 1)
        def _():
            self._rs1(k).start()

    def event1(self):
        for k in T3:
            self._rs1(k).wait_recv()
            s = self._half(k, 1, QUART)
            for o, go in ((QUART - s, True), (s, False)):
                for b in T3:
                    self.p[self._at(k, b, o, QUART), :] += self.r1[k, pl.ds(_mul(b * Q + o, 8), QUART), :]
                    if go:
                        self._rs2(k, b).start()

    def event2(self):
        for k in T3:
            s, t = self._half(k, 1, QUART), self._half(k, 2, EIGHTH)
            for b in T3:
                self._rs2(k, b).wait_recv()
            for o, go in ((EIGHTH - t, True), (t, False)):
                for b in T3:
                    self.p[self._at(k, b, s + o, EIGHTH), :] += self.r2[k, b, pl.ds(_mul(o, 8), EIGHTH), :]
                    if go:
                        self._rs3(k, b).start()

    def event3(self, f):
        for k, b in KB:
            self._rs3(k, b).wait_recv()
            f[k, b] = self.p[self._at(k, b, self._half(k, 1, QUART) + self._half(k, 2, EIGHTH), EIGHTH), :] + self.r3[k, b]

    def sent(self):
        for i in range(6):
            self._d2d(i).wait_send()

    def finish(self):
        for k in T3:
            self._rs1(k).wait_send()
        for k, b in KB:
            self._rs2(k, b).wait_send()
            self._rs3(k, b).wait_send()


def _ag_scratch():
    return [DMA((3,))] * 7 + [DMA((3, 3))] * 4


class _Gather:
    def __init__(self, place, f, out, sems):
        self.pl, self.f, self.out = place, f, out
        self.loc, self.s1, self.r1, self.s2, self.r2, self.fas, self.far, self.s3, self.r3, self.fbs, self.fbr = sems

    def _rows(self, k, depth):
        o, n = self.pl.core * 2 * Q, 2 * Q
        for d in range(depth):
            n = n // 2
            o = o + self.pl.bit((k + d) % 3) * n
        return pl.ds(_mul(o, 8), n)

    def _at(self, k, depth):
        return self.out.at[k, :, self._rows(k, depth), :]

    def _local(self, k):
        return pltpu.make_async_copy(self.f.at[k], self._at(k, 3), self.loc.at[k])

    def _c1(self, k):
        return _rcopy(self.f.at[k], self._at(k, 3), self.s1.at[k], self.r1.at[k], self.pl.across((k + 2) % 3))

    def _c2(self, k):
        r = self._at(k, 2)
        return _rcopy(r, r, self.s2.at[k], self.r2.at[k], self.pl.across((k + 1) % 3))

    def _c3(self, k, b):
        r = self.out.at[k, b, self._rows(k, 1), :]
        return _rcopy(r, r, self.s3.at[k, b], self.r3.at[k, b], self.pl.across(k))

    def _fa(self, k):
        r = self._at(k, 1)
        return _rcopy(r, r, self.fas.at[k], self.far.at[k], self.pl.partner())

    def _fb(self, k, b):
        o = self.pl.core * 2 * Q + (1 - self.pl.bit(k)) * Q
        r = self.out.at[k, b, pl.ds(_mul(o, 8), Q), :]
        return _rcopy(r, r, self.fbs.at[k, b], self.fbr.at[k, b], self.pl.partner())

    def start(self):
        for k in T3:
            self._c1(k).start()
            self._local(k).start()

    def event1(self):
        for k in T3:
            self._local(k).wait()
            self._c1(k).wait_recv()
            self._c2(k).start()

    def event2(self):
        for k in T3:
            self._c2(k).wait_recv()
            for b in T3:
                self._c3(k, b).start()
            self._fa(k).start()

    def event3(self):
        for b in T3:
            for k in T3:
                self._c3(k, b).wait_recv()
                self._fb(k, b).start()

    def finish(self):
        for k in T3:
            self._c1(k).wait_send()
            self._c2(k).wait_send()
            self._fa(k).wait()
        for k, b in KB:
            self._c3(k, b).wait_send()
            self._fb(k, b).wait()


def _k2(cnt, gcat_i, zt_i, a_i, stat, gamma, beta, w2, w1, xt, x, z, g, dw1_o, dw2_o, y_o, dx_o, t_o,
        cat, lt, av, wv, zv, sums, ebuf, ess, ers, dsem, esem, f1, f2, *sc):
    sc = list(sc)

    def take(group):
        n = len(group)
        out, sc[:n] = sc[:n], []
        return out
    place = _Place()
    hd, hz = _Halo(av, take(_halo_scratch())), _Halo(zv, take(_halo_scratch()))
    bufs = take(_rs_buffers())
    rs2, rs1 = _Scatter(place, bufs, take(_rs_scratch())), _Scatter(place, bufs, take(_rs_scratch()))
    ag2, ag1 = _Gather(place, f2, dw2_o, take(_ag_scratch())), _Gather(place, f1, dw1_o, take(_ag_scratch()))
    dn = bufs[0]
    ins = _load(((zt_i, lt), (gcat_i, cat), (w2, wv), (a_i, av), (z, zv)), dsem)
    sums[...] = jnp.zeros_like(sums)
    ins[0].wait()
    ins[1].wait()

    @pl.loop(0, 12)
    def _(j):
        rs2.block(j, lt, cat)
    for c in ins[2:]:
        c.wait()
    cxt, = _load(((xt, lt),), esem)
    hz.start()
    rs2.sent()

    def dz_block(i, m0, m):
        dn[m, :] = _conv_t(cat, wv, m0, 512)
        for q in (2 * i, 2 * i + 1):
            for s in LANES:
                mm = _rows(q, TW)
                xh = (av[mm, s].astype(F32) - stat[0:1, s]) * stat[1:2, s]
                nn = xh * gamma[:, s] + beta[:, s]
                n2, t = _gelu_parts(nn)
                d = dn[mm, s] * (0.5 * (1.0 + t) + (0.5 * GC) * nn * (1.0 - t * t) * (1.0 + (3.0 * GA) * n2))
                dn[mm, s] = d
                sums[0:1, s] += jnp.sum(d * xh, axis=0, keepdims=True)
                sums[1:2, s] += jnp.sum(d, axis=0, keepdims=True)

        @pl.when(i == 2)
        def _():
            rs2.event1()
    _blocks(dz_block)
    cw1, = _load(((w1, wv),), dsem)
    ebuf[0] = jnp.zeros((16, 128), F32)
    for k, l in enumerate(LANES):
        for s in (0, 1):
            ebuf[0, s * 8 + k:s * 8 + k + 1, :] = sums[s:s + 1, l]
    tot = _exchange_sum(ebuf, _exchange(ebuf, ess, ers))
    for k, l in enumerate(LANES):
        for s in (0, 1):
            sums[s:s + 1, l] = tot[s * 8 + k:s * 8 + k + 1, :]
    t_o[...] = sums[...]
    down, up = _group_mats()
    sums[...] = _dotf(_dotf(sums[...] * gamma[...], down) * (1.0 / cnt), up)

    def da_tile(m, s):
        xh = (av[m, s].astype(F32) - stat[0:1, s]) * stat[1:2, s]
        av[m, s] = (stat[1:2, s] * (dn[m, s] * gamma[:, s] - sums[1:2, s] - xh * sums[0:1, s])).astype(BF)
    _tiles(da_tile)
    hd.start()
    rs2.event2()
    hd.wait_cols()
    hd.centers(cat)
    hd.wait_rows()
    hd.borders(cat)
    cgv, = _load(((g, av),), dsem.at[pl.ds(1, 1)])
    rs2.event3(f2)
    ag2.start()
    rs2.finish()
    cxt.wait()

    @pl.loop(0, 12)
    def _(j):
        rs1.block(j, lt, cat)

        @pl.when(j == 4)
        def _():
            ag2.event1()
    cw1.wait()
    cgv.wait()

    def dx_block(i, m0, m):
        av[m, :] = (_conv_t(cat, wv, m0, 512) + av[m, :].astype(F32)).astype(BF)

        @pl.when(i == 2)
        def _():
            rs1.event1()
            ag2.event2()
    _blocks(dx_block)
    cdx, cw2 = _load(((av, dx_o), (w2, wv)), dsem)
    hz.wait_cols()
    hz.centers(cat)
    hz.wait_rows()
    hz.borders(cat)
    cxv, = _load(((x, zv),), esem)
    rs1.event2()
    cw2.wait()
    cxv.wait()

    def y_block(i, m0, m):
        zv[m, :] = (_conv(cat, wv, m0, 512) + zv[m, :].astype(F32)).astype(BF)

        @pl.when(i == 2)
        def _():
            rs1.event3(f1)
            ag1.start()
    _blocks(y_block)
    cy, = _load(((zv, y_o),), esem)
    ag1.event1()
    ag2.event3()
    ag1.event2()
    cdx.wait()
    cy.wait()
    rs1.sent()
    rs1.finish()
    ag2.finish()
    ag1.event3()
    ag1.finish()


def _params(**kw):
    return pltpu.CompilerParams(has_side_effects=True, vmem_limit_bytes=64 * 2**20 - 65536, **kw)


def solution(mesh):
    tile = P(None, 'h', 'w', None)
    cnt = float(TH * TW * 16 * (C // GROUPS))
    sds = jax.ShapeDtypeStruct
    V = pltpu.VMEM

    def body(x, w1, gamma, beta, w2, g):
        x2, g2 = x.reshape(PIX, C), g.reshape(PIX, C)
        w1r, w2r = w1.reshape(3, 3 * C, C), w2.reshape(3, 3 * C, C)
        ga, be = gamma.reshape(1, C), beta.reshape(1, C)
        tile, flip, wide, wts = sds((PIX, C), BF), sds((C, PIX), BF), sds((10 * TW, 3 * C), BF), sds((3, 3 * C, C), BF)
        dw = sds((3, 3, C, C), F32)
        vm = lambda l: [V(a.shape, a.dtype) for a in l]
        sums = [V((8, C), F32)]
        sems = [DMA((16,)), DMA((16,)), DMA((8,)), DMA((2,))]
        gcat, a, z, zt, xt, stat = pl.pallas_call(
            lambda *r: _k1(cnt, *r),
            out_shape=[wide, tile, tile, flip, flip, sds((8, C), F32)],
            in_specs=[ANY] * 3 + [VM] * 2, out_specs=[ANY] * 5 + [VM],
            scratch_shapes=vm((tile, tile, wts, wide, wide, tile, tile, flip, flip)) + sums + [V((16, 8, 128), F32)] + sems + _halo_scratch() * 2,
            compiler_params=_params(), name='k1')(x2, w1r, g2, ga, be)
        dw1, dw2, y, dx, t = pl.pallas_call(
            lambda *r: _k2(cnt, *r),
            out_shape=[dw, dw, tile, tile, sds((8, C), F32)],
            in_specs=[ANY] * 3 + [VM] * 3 + [ANY] * 6, out_specs=[ANY] * 4 + [VM],
            scratch_shapes=vm((wide, flip, tile, wts, tile)) + sums + [V((16, 16, 128), F32)] + sems + [V((3, 3, EIGHTH, C), F32)] * 2
            + _halo_scratch() * 2 + _rs_buffers() + _rs_scratch() * 2 + _ag_scratch() * 2,
            compiler_params=_params(), name='k2')(gcat, zt, a, stat, ga, be, w2r, w1r, xt, x2, z, g2)
        return y.reshape(x.shape), dx.reshape(x.shape), dw1, dw2, t[0], t[1]

    return jax.shard_map(body, mesh=mesh, in_specs=(tile, P(), P(), P(), P(), tile), out_specs=(tile, tile, P(), P(), P(), P()), check_vma=False)
```

time: 525 us -> 325 us (0.62)
  waiting for transfers between devices: 287 us -> 0 us
  Pallas kernels: 191 us -> 292 us
  between operations: 14.1 us -> 0.65 us
    psum x1 -> x0, waiting for transfers between devices: 287 us -> none  [body(): dw1 = lax.psum(dw1p, ('h', 'w'))]
    pallas_call x3 -> x2, Pallas kernels: 191 us -> 292 us  [the longest x1 233 us: body(): pl.pallas_call(lambda *r: _k2(cnt, *r), out_shape=[dw, dw, tile, tile, sd...]
    unnamed x8 -> x6, local copies, waits for them, and re-layouts: 27.5 us -> 28.4 us
  transfers between devices with their start and end apart: 1 -> 0, of which waited for: 1 -> 0; matrix products, arithmetic and copies ran while one was open for 0% -> 0% of each run, Pallas kernels for 0% -> 0%
where the time goes in v2:
time: 325 us
  Pallas kernels  292 us (90%)
  local copies, waits for them, and re-layouts  32.4 us (10%)
    pallas_call x1, Pallas kernels, body(): pl.pallas_call(lambda *r: _k2(cnt, *r), out_shape=[dw, dw, tile, tile, sd...  233 us
    pallas_call x1, Pallas kernels, body(): pl.pallas_call(lambda *r: _k1(cnt, *r), out_shape=[wide, tile, tile, flip...  58.8 us
    unnamed x6, local copies, waits for them, and re-layouts  28.4 us

profile of v2, /device:TPU:0, one launch (start us, length us, event | category | flops | bytes accessed | tf_op | source)
XLA Modules:
  0.0 324.6 jit_solution(7988436668267992725)
XLA Ops:
  0.6 1.3 reshape.39.r_3_.r_4_
  1.9 1.3 reshape.40.r_4_.r_5_
  3.2 58.8 %k1.1 = (bf16[2560,1920]{1,0:T(8,128)(2,1)}, bf16[2048,640]{1,0:T(8,128)(2,1)}, bf16[2048,640]{1,0:T(8,128)(2,1)}, bf16[640,2048]{1,0:T(8,128)(2,1)}, bf16[640,2048]{1,0:T(8,128)(2,1)}, /*index=5*/f32[8,640]{1,0:T(8,128)}) custom-call(bf16[2048,640]{1,0:T(8,128)(2,1)} %bitcast.8, bf16[3,1920,640]{2,1,0:T(8,128)(2,1)} %bitcast.6, bf16[2048,640]{1,0:T(8,128)(2,1)} %bitcast.10, ...), custom_call_target="tpu_custom_call" | custom-call | tf_op jit(solution)/shard_map/k1/pallas_call | solution.py:650
  62.0 232.7 %k2.1 = (f32[3,3,640,640]{3,2,1,0:T(8,128)}, f32[3,3,640,640]{3,2,1,0:T(8,128)}, bf16[2048,640]{1,0:T(8,128)(2,1)}, bf16[2048,640]{1,0:T(8,128)(2,1)}, f32[8,640]{1,0:T(8,128)}) custom-call(bf16[2560,1920]{1,0:T(8,128)(2,1)} %get-tuple-element.17.r_0_, bf16[640,2048]{1,0:T(8,128)(2,1)} %get-tuple-element.18.r_1_, bf16[2048,640]{1,0:T(8,128)(2,1)} %get-tuple-element.19.r_2_, ...), custom_call_target="tpu_custom_call" | custom-call | tf_op jit(solution)/shard_map/k2/pallas_call | solution.py:656
  294.7 1.4 slice_reduce_fusion
  296.1 0.0 copy-start
  296.1 3.7 %copy.16 = bf16[1,8,256,640]{3,2,1,0:T(8,128)(2,1)} copy(bf16[1,8,256,640]{3,2,1,0:T(8,128)(2,1)} %bitcast.14) | data formatting | bytes 5242880
  299.8 0.0 copy-done
  299.8 1.5 copy.17
  301.3 11.6 %copy.18 = f32[3,3,640,640]{3,2,1,0:T(8,128)} copy(f32[3,3,640,640]{3,2,1,0:T(8,128)} %get-tuple-element.38) | data formatting | bytes 29491200
  312.9 11.6 %copy.19 = f32[3,3,640,640]{3,2,1,0:T(8,128)} copy(f32[3,3,640,640]{3,2,1,0:T(8,128)} %get-tuple-element.39) | data formatting | bytes 29491200
Async XLA Ops:
  296.1 3.7 %copy-start = (bf16[2048,640]{1,0:T(8,128)(2,1)S(1)}, bf16[2048,640]{1,0:T(8,128)(2,1)}, u32[]{:S(2)}) copy-start(bf16[2048,640]{1,0:T(8,128)(2,1)} %get-tuple-element.24) | copy-start | bytes 7864324

commit v3 on v2

--- a/solution.py
+++ b/solution.py
@@ -421,9 +421,11 @@
         for i in range(6):
             self._d2d(i).wait_send()
 
-    def finish(self):
+    def sent1(self):
         for k in T3:
             self._rs1(k).wait_send()
+
+    def finish(self):
         for k, b in KB:
             self._rs2(k, b).wait_send()
             self._rs3(k, b).wait_send()
@@ -434,8 +436,8 @@
 
 
 class _Gather:
-    def __init__(self, place, f, out, sems):
-        self.pl, self.f, self.out = place, f, out
+    def __init__(self, place, f, out, sems, vmem=False):
+        self.pl, self.f, self.out, self.vmem = place, f, out, vmem
         self.loc, self.s1, self.r1, self.s2, self.r2, self.fas, self.far, self.s3, self.r3, self.fbs, self.fbr = sems
 
     def _rows(self, k, depth):
@@ -451,6 +453,12 @@
     def _local(self, k):
         return pltpu.make_async_copy(self.f.at[k], self._at(k, 3), self.loc.at[k])
 
+    def _local_start(self, k):
+        if self.vmem:
+            self.out[k, :, self._rows(k, 3), :] = self.f[k]
+        else:
+            self._local(k).start()
+
     def _c1(self, k):
         return _rcopy(self.f.at[k], self._at(k, 3), self.s1.at[k], self.r1.at[k], self.pl.across((k + 2) % 3))
 
@@ -474,20 +482,23 @@
     def start(self):
         for k in T3:
             self._c1(k).start()
-            self._local(k).start()
+            self._local_start(k)
 
     def event1(self):
         for k in T3:
-            self._local(k).wait()
+            if not self.vmem:
+                self._local(k).wait()
             self._c1(k).wait_recv()
             self._c2(k).start()
 
-    def event2(self):
+    def event2(self, part=T3):
         for k in T3:
-            self._c2(k).wait_recv()
-            for b in T3:
+            if 0 in part:
+                self._c2(k).wait_recv()
+            for b in part:
                 self._c3(k, b).start()
-            self._fa(k).start()
+            if 0 in part:
+                self._fa(k).start()
 
     def event3(self):
         for b in T3:
@@ -505,8 +516,8 @@
             self._fb(k, b).wait()
 
 
-def _k2(cnt, gcat_i, zt_i, a_i, stat, gamma, beta, w2, w1, xt, x, z, g, dw1_o, dw2_o, y_o, dx_o, t_o,
-        cat, lt, av, wv, zv, sums, ebuf, ess, ers, dsem, esem, f1, f2, *sc):
+def _k2(cnt, gcat_i, zt_i, a_i, stat, gamma, beta, w2, w1, xt, x, z, g, dw2_o, y_o, dx_o, f1, t_o,
+        cat, lt, av, wv, zv, sums, ebuf, ess, ers, dsem, esem, f2, *sc):
     sc = list(sc)
 
     def take(group):
@@ -517,7 +528,7 @@
     hd, hz = _Halo(av, take(_halo_scratch())), _Halo(zv, take(_halo_scratch()))
     bufs = take(_rs_buffers())
     rs2, rs1 = _Scatter(place, bufs, take(_rs_scratch())), _Scatter(place, bufs, take(_rs_scratch()))
-    ag2, ag1 = _Gather(place, f2, dw2_o, take(_ag_scratch())), _Gather(place, f1, dw1_o, take(_ag_scratch()))
+    ag2 = _Gather(place, f2, dw2_o, take(_ag_scratch()))
     dn = bufs[0]
     ins = _load(((zt_i, lt), (gcat_i, cat), (w2, wv), (a_i, av), (z, zv)), dsem)
     sums[...] = jnp.zeros_like(sums)
@@ -574,28 +585,31 @@
     hd.wait_rows()
     hd.borders(cat)
     cgv, = _load(((g, av),), dsem.at[pl.ds(1, 1)])
-    rs2.event3(f2)
-    ag2.start()
-    rs2.finish()
+    rs2.sent1()
     cxt.wait()
 
     @pl.loop(0, 12)
     def _(j):
         rs1.block(j, lt, cat)
 
-        @pl.when(j == 4)
+        @pl.when(j == 2)
+        def _():
+            rs2.event3(f2)
+            ag2.start()
+
+        @pl.when(j == 7)
         def _():
             ag2.event1()
+            rs2.finish()
     cw1.wait()
     cgv.wait()
 
     def dx_block(i, m0, m):
         av[m, :] = (_conv_t(cat, wv, m0, 512) + av[m, :].astype(F32)).astype(BF)
 
-        @pl.when(i == 2)
+        @pl.when(i == 3)
         def _():
             rs1.event1()
-            ag2.event2()
     _blocks(dx_block)
     cdx, cw2 = _load(((av, dx_o), (w2, wv)), dsem)
     hz.wait_cols()
@@ -603,33 +617,48 @@
     hz.wait_rows()
     hz.borders(cat)
     cxv, = _load(((x, zv),), esem)
-    rs1.event2()
     cw2.wait()
     cxv.wait()
 
     def y_block(i, m0, m):
         zv[m, :] = (_conv(cat, wv, m0, 512) + zv[m, :].astype(F32)).astype(BF)
 
-        @pl.when(i == 2)
-        def _():
-            rs1.event3(f1)
-            ag1.start()
+        @pl.when(i == 1)
+        def _():
+            ag2.event2((0,))
+
+        @pl.when(i == 3)
+        def _():
+            rs1.event2()
+            ag2.event2((1, 2))
     _blocks(y_block)
     cy, = _load(((zv, y_o),), esem)
-    ag1.event1()
+    rs1.event3(f1)
     ag2.event3()
-    ag1.event2()
     cdx.wait()
     cy.wait()
     rs1.sent()
+    rs1.sent1()
     rs1.finish()
     ag2.finish()
+
+
+def _k3(f1, dw1_o, *sems):
+    ag1 = _Gather(_Place(), f1, dw1_o, sems, True)
+    ag1.start()
+    ag1.event1()
+    ag1.event2()
     ag1.event3()
     ag1.finish()
 
 
-def _params(**kw):
-    return pltpu.CompilerParams(has_side_effects=True, vmem_limit_bytes=64 * 2**20 - 65536, **kw)
+def _k4(dw1, dw2, y, dx, dw1_o, dw2_o, y_o, dx_o, dsem):
+    for c in _load(((dw1, dw1_o), (dw2, dw2_o), (y, y_o), (dx, dx_o)), dsem):
+        c.wait()
+
+
+def _params(mib=64):
+    return pltpu.CompilerParams(has_side_effects=True, vmem_limit_bytes=mib * 2**20 - 65536)
 
 
 def solution(mesh):
@@ -653,13 +682,21 @@
             in_specs=[ANY] * 3 + [VM] * 2, out_specs=[ANY] * 5 + [VM],
             scratch_shapes=vm((tile, tile, wts, wide, wide, tile, tile, flip, flip)) + sums + [V((16, 8, 128), F32)] + sems + _halo_scratch() * 2,
             compiler_params=_params(), name='k1')(x2, w1r, g2, ga, be)
-        dw1, dw2, y, dx, t = pl.pallas_call(
+        piece = sds((3, 3, EIGHTH, C), F32)
+        dw2, y, dx, f1, t = pl.pallas_call(
             lambda *r: _k2(cnt, *r),
-            out_shape=[dw, dw, tile, tile, sds((8, C), F32)],
-            in_specs=[ANY] * 3 + [VM] * 3 + [ANY] * 6, out_specs=[ANY] * 4 + [VM],
-            scratch_shapes=vm((wide, flip, tile, wts, tile)) + sums + [V((16, 16, 128), F32)] + sems + [V((3, 3, EIGHTH, C), F32)] * 2
-            + _halo_scratch() * 2 + _rs_buffers() + _rs_scratch() * 2 + _ag_scratch() * 2,
+            out_shape=[dw, tile, tile, piece, sds((8, C), F32)],
+            in_specs=[ANY] * 3 + [VM] * 3 + [ANY] * 6, out_specs=[ANY] * 3 + [VM] * 2,
+            scratch_shapes=vm((wide, flip, tile, wts, tile)) + sums + [V((16, 16, 128), F32)] + sems + vm((piece,))
+            + _halo_scratch() * 2 + _rs_buffers() + _rs_scratch() * 2 + _ag_scratch(),
             compiler_params=_params(), name='k2')(gcat, zt, a, stat, ga, be, w2r, w1r, xt, x2, z, g2)
+        dw1 = pl.pallas_call(
+            _k3, out_shape=dw, in_specs=[VM], out_specs=VM,
+            scratch_shapes=_ag_scratch(),
+            compiler_params=_params(2), name='k3')(f1)
+        dw1, dw2, y, dx = pl.pallas_call(
+            _k4, out_shape=[dw, dw, tile, tile], in_specs=[VM] * 4, out_specs=[ANY] * 4,
+            scratch_shapes=sems[2:3], compiler_params=pltpu.CompilerParams(vmem_limit_bytes=2**20), name='k4')(dw1, dw2, y, dx)
         return y.reshape(x.shape), dx.reshape(x.shape), dw1, dw2, t[0], t[1]
 
     return jax.shard_map(body, mesh=mesh, in_specs=(tile, P(), P(), P(), P(), tile), out_specs=(tile, tile, P(), P(), P(), P()), check_vma=False)

time: 325 us -> 323 us (level)
  local copies, waits for them, and re-layouts: 32.4 us -> 8.61 us
  Pallas kernels: 292 us -> 313 us
    unnamed x6 -> x8, local copies, waits for them, and re-layouts: 28.4 us -> 4.66 us
    pallas_call x1 -> x3, Pallas kernels: 233 us -> 254 us  [the longest x1 184 us: body(): pl.pallas_call(lambda *r: _k2(cnt, *r), out_shape=[dw, tile, tile, piece,...]
where the time goes in v3:
time: 323 us; the launch traced here: 322 us
  Pallas kernels  313 us (97%)
  local copies, waits for them, and re-layouts  8.61 us (3%)
    pallas_call x1, Pallas kernels, body(): pl.pallas_call(lambda *r: _k2(cnt, *r), out_shape=[dw, tile, tile, piece,...  184 us
    pallas_call x1, Pallas kernels, body(): pl.pallas_call(lambda *r: _k1(cnt, *r), out_shape=[wide, tile, tile, flip...  58.8 us
    pallas_call x1, Pallas kernels, body(): pl.pallas_call(_k3, out_shape=dw, in_specs=[VM], out_specs=VM, scratch_sh...  57.9 us
    pallas_call x1, Pallas kernels, body(): pl.pallas_call(_k4, out_shape=[dw, dw, tile, tile], in_specs=[VM] * 4, ou...  11.6 us

profile of v3, /device:TPU:0, one launch (start us, length us, event | category | flops | bytes accessed | tf_op | source)
XLA Modules:
  0.0 322.2 jit_solution(16645136150457159871)
XLA Ops:
  0.6 1.3 reshape.39.r_3_.r_4_
  1.9 1.3 reshape.40.r_4_.r_5_
  3.2 58.8 %k1.1 = (bf16[2560,1920]{1,0:T(8,128)(2,1)}, bf16[2048,640]{1,0:T(8,128)(2,1)}, bf16[2048,640]{1,0:T(8,128)(2,1)}, bf16[640,2048]{1,0:T(8,128)(2,1)}, bf16[640,2048]{1,0:T(8,128)(2,1)}, /*index=5*/f32[8,640]{1,0:T(8,128)}) custom-call(bf16[2048,640]{1,0:T(8,128)(2,1)} %bitcast.8, bf16[3,1920,640]{2,1,0:T(8,128)(2,1)} %bitcast.6, bf16[2048,640]{1,0:T(8,128)(2,1)} %bitcast.10, ...), custom_call_target="tpu_custom_call" | custom-call | tf_op jit(solution)/shard_map/k1/pallas_call | solution.py:679
  62.0 184.4 %k2.1 = (f32[3,3,640,640]{3,2,1,0:T(8,128)}, bf16[2048,640]{1,0:T(8,128)(2,1)}, bf16[2048,640]{1,0:T(8,128)(2,1)}, f32[3,3,40,640]{3,2,1,0:T(8,128)}, f32[8,640]{1,0:T(8,128)}) custom-call(bf16[2560,1920]{1,0:T(8,128)(2,1)} %get-tuple-element.21.r_0_, bf16[640,2048]{1,0:T(8,128)(2,1)} %get-tuple-element.22.r_1_, bf16[2048,640]{1,0:T(8,128)(2,1)} %get-tuple-element.23.r_2_, ...), custom_call_target="tpu_custom_call" | custom-call | tf_op jit(solution)/shard_map/k2/pallas_call | solution.py:686
  246.4 1.4 slice_reduce_fusion
  247.8 0.0 copy-start.3
  247.8 1.2 copy-done.3
  249.0 0.0 copy-start
  249.0 57.9 %k3.1.dw1 = f32[3,3,640,640]{3,2,1,0:T(8,128)S(1)} custom-call(f32[3,3,40,640]{3,2,1,0:T(8,128)S(1)} %copy-done.3), custom_call_target="tpu_custom_call" | custom-call | tf_op jit(solution)/shard_map/k3/pallas_call | solution.py:693
  306.9 0.0 copy-done
  306.9 0.0 copy-start.1
  306.9 1.7 copy-done.1
  308.6 0.0 copy-start.2
  308.6 1.7 copy-done.2
  310.4 11.6 %k4.1 = (f32[3,3,640,640]{3,2,1,0:T(8,128)}, f32[3,3,640,640]{3,2,1,0:T(8,128)}, bf16[2048,640]{1,0:T(8,128)(2,1)}, bf16[2048,640]{1,0:T(8,128)(2,1)}) custom-call(f32[3,3,640,640]{3,2,1,0:T(8,128)S(1)} %k3.1.dw1, f32[3,3,640,640]{3,2,1,0:T(8,128)S(1)} %copy-done, bf16[2048,640]{1,0:T(8,128)(2,1)S(1)} %copy-done.1, bf16[2048,640]{1,0:T(8,128)(2,1)S(1)} %copy-done.2), custom_call_target="tpu_custom_call" | custom-call | tf_op jit(solution)/shard_map/k4/pallas_call | solution.py:697
Async XLA Ops:
  247.8 1.2 copy-start.3
  249.0 57.9 %copy-start = (f32[3,3,640,640]{3,2,1,0:T(8,128)S(1)}, f32[3,3,640,640]{3,2,1,0:T(8,128)}, u32[]{:S(2)}) copy-start(f32[3,3,640,640]{3,2,1,0:T(8,128)} %get-tuple-element.28.dw2) | copy-start | bytes 44236804
  306.9 1.7 copy-start.1
  308.6 1.7 copy-start.2
